TPU v7x, 32 devices: a whole 2x2x4 slice. The times are simulated.
32 devices in a mesh: vel: 8 (over z, x), space: 4 (over y, core).
Axes of the slice: x: 2, y: 2, z: 4, core: 2. Of those that a mesh axis runs over, the one named last changes fastest.
Arguments:
- distribution: float32 [16384, 16, 256], P('vel', 'space'), may hold values from 0 to 5, as said below
- block_map: int32 [128], P('vel'), may hold values from 0 to 127, as said below
- inflow_mask: int32 [16, 256], P('space'), may hold values 0 or 1
- owner_map: int32 [8], replicated, may hold values from 0 to 7, each once
- inflow_scalars: float32 [2], replicated, may hold values from 0.8 to 1.25
- inflow_drift: float32 [3], replicated, may hold values from -0.3 to 0.3
Outputs:
- new_distribution: float32 [16384, 16, 256], P('vel', 'space')
- macro_fields: float32 [5, 4096], P(None, ('space', 'vel'))
Inputs may be any that keep to these rules, and one draw needn't show every extreme that they name: `block_map`: a permutation of the velocity blocks. `owner_map`: a permutation of the owner positions. `distribution`: every entry is positive.
All inputs are finite; a program needn't handle non-finite values. No bound on the sum of `inflow_mask` on one device may be relied on, other than what follows from the above.
Results may differ from a plain program's by a relative error of at most 0.0001.
Values sent between devices are 32-bit elements; how exact they have to be, the bound alone decides.
No kernel may reach another device: no remote copies, remote signals or barrier semaphores. Data moves between devices by JAX's collectives and lax.ppermute only.
A program may use at most 192 MiB of HBM per device.

v0:
```python
import math

import jax
import jax.numpy as jnp
from jax import lax
from jax.sharding import PartitionSpec as P

NVX = 32
NVY = 32
NVZ = 16
VB = 128
NZ = 16
MSTEPS = 4


SPEED_LIMIT = 3.5
PRANDTL = 2.0 / 3.0
KINETIC_STEP = 0.12
VISCOSITY_REF = 0.25
VISCOSITY_POWER = 0.81
MACRO_STEP = 0.1
DIFFUSION = 1.6
HIGHEST = lax.Precision.HIGHEST


def extended(array, sides, width):
    for axis, dim in sides:
        devices, length = (lax.axis_size(axis), array.shape[dim])
        up = [(i, (i + 1) % devices) for i in range(devices - 1)]
        down = [(j, i) for i, j in up]
        last = lax.slice_in_dim(array, length - width, length, axis=dim)
        initial = lax.slice_in_dim(array, 0, width, axis=dim)
        before = lax.ppermute(last, axis, up)
        after = lax.ppermute(initial, axis, down)
        array = jnp.concatenate([before, array, after], axis=dim)
    return array


def coordinates(node_ids):
    along_x = node_ids // (NVY * NVZ)
    along_y = node_ids // NVZ % NVY
    along_z = node_ids % NVZ
    speed_x = -SPEED_LIMIT + (along_x.astype(jnp.float32) + 0.5) * (2.0 * SPEED_LIMIT / NVX)
    speed_y = -SPEED_LIMIT + (along_y.astype(jnp.float32) + 0.5) * (2.0 * SPEED_LIMIT / NVY)
    speed_z = -SPEED_LIMIT + (along_z.astype(jnp.float32) + 0.5) * (2.0 * SPEED_LIMIT / NVZ)
    return (speed_x, speed_y, speed_z)


def moment_rows(speed_x, speed_y, speed_z):
    weight = (
        2.0
        * SPEED_LIMIT
        / NVX
        * (2.0 * SPEED_LIMIT / NVY)
        * (2.0 * SPEED_LIMIT / NVZ)
        / (2.0 * math.pi) ** 1.5
    )
    square = speed_x * speed_x + speed_y * speed_y + speed_z * speed_z
    unity = jnp.ones_like(speed_x)
    return weight * jnp.stack(
        [
            unity,
            speed_x,
            speed_y,
            speed_z,
            square,
            speed_x * speed_x,
            speed_y * speed_y,
            speed_x * speed_y,
            speed_x * speed_z,
            speed_y * speed_z,
            speed_x * square,
            speed_y * square,
            speed_z * square,
        ]
    )


def convert(moments):
    density = moments[0]
    vel_x = moments[1] / density
    vel_y = moments[2] / density
    vel_z = moments[3] / density
    twice_energy = moments[4]
    speed_sq = vel_x * vel_x + vel_y * vel_y + vel_z * vel_z
    temper = (twice_energy / density - speed_sq) / 3.0
    pressure = density * temper
    press_xx = moments[5]
    press_yy = moments[6]
    press_xy = moments[7]
    press_xz = moments[8]
    press_yz = moments[9]
    press_zz = twice_energy - press_xx - press_yy
    stress_xx = press_xx - density * vel_x * vel_x - pressure
    stress_yy = press_yy - density * vel_y * vel_y - pressure
    stress_xy = press_xy - density * vel_x * vel_y
    stress_xz = press_xz - density * vel_x * vel_z
    stress_yz = press_yz - density * vel_y * vel_z
    heat_x = 0.5 * (
        moments[10]
        - 2.0 * (vel_x * press_xx + vel_y * press_xy + vel_z * press_xz)
        - vel_x * twice_energy
        + 2.0 * density * vel_x * speed_sq
    )
    heat_y = 0.5 * (
        moments[11]
        - 2.0 * (vel_x * press_xy + vel_y * press_yy + vel_z * press_yz)
        - vel_y * twice_energy
        + 2.0 * density * vel_y * speed_sq
    )
    heat_z = 0.5 * (
        moments[12]
        - 2.0 * (vel_x * press_xz + vel_y * press_yz + vel_z * press_zz)
        - vel_z * twice_energy
        + 2.0 * density * vel_z * speed_sq
    )
    return jnp.stack(
        [
            density,
            moments[1],
            moments[2],
            moments[3],
            0.5 * twice_energy,
            stress_xx,
            stress_yy,
            stress_xy,
            stress_xz,
            stress_yz,
            heat_x,
            heat_y,
            heat_z,
        ]
    )


def roll_z(values, offset):
    position = jnp.arange(values.shape[-1]) % NZ
    if offset == 1:
        return jnp.where(
            position == 0, jnp.roll(values, 1 - NZ, axis=-1), jnp.roll(values, 1, axis=-1)
        )
    return jnp.where(
        position == NZ - 1, jnp.roll(values, NZ - 1, axis=-1), jnp.roll(values, -1, axis=-1)
    )


def macro_step(state, extra):
    density = state[0]
    vel_x = state[1] / density
    vel_y = state[2] / density
    vel_z = state[3] / density
    energy = state[4]
    temper = 2.0 / 3.0 * (energy / density - 0.5 * (vel_x * vel_x + vel_y * vel_y + vel_z * vel_z))
    pressure = density * temper
    stress_xx, stress_yy, stress_xy, stress_xz, stress_yz = (
        extra[0],
        extra[1],
        extra[2],
        extra[3],
        extra[4],
    )
    stress_zz = -stress_xx - stress_yy
    enthalpy = energy + pressure
    flux_x = jnp.stack(
        [
            state[1],
            state[1] * vel_x + pressure + stress_xx,
            state[2] * vel_x + stress_xy,
            state[3] * vel_x + stress_xz,
            enthalpy * vel_x + stress_xx * vel_x + stress_xy * vel_y + stress_xz * vel_z + extra[5],
        ]
    )
    flux_y = jnp.stack(
        [
            state[2],
            state[1] * vel_y + stress_xy,
            state[2] * vel_y + pressure + stress_yy,
            state[3] * vel_y + stress_yz,
            enthalpy * vel_y + stress_xy * vel_x + stress_yy * vel_y + stress_yz * vel_z + extra[6],
        ]
    )
    flux_z = jnp.stack(
        [
            state[3],
            state[1] * vel_z + stress_xz,
            state[2] * vel_z + stress_yz,
            state[3] * vel_z + pressure + stress_zz,
            enthalpy * vel_z + stress_xz * vel_x + stress_yz * vel_y + stress_zz * vel_z + extra[7],
        ]
    )
    div_x = 0.5 * (flux_x[:, 2:] - flux_x[:, :-2])
    div_y = 0.5 * (jnp.roll(flux_y, -NZ, axis=-1) - jnp.roll(flux_y, NZ, axis=-1))[:, 1:-1]
    div_z = 0.5 * (roll_z(flux_z, -1) - roll_z(flux_z, 1))[:, 1:-1]
    center = state[:, 1:-1]
    beside = (
        jnp.roll(state, -NZ, axis=-1)
        + jnp.roll(state, NZ, axis=-1)
        + roll_z(state, -1)
        + roll_z(state, 1)
    )[:, 1:-1]
    spread = state[:, 2:] + state[:, :-2] + beside - 6.0 * center
    return center - MACRO_STEP * (div_x + div_y + div_z) + DIFFUSION * MACRO_STEP * spread


def equilibrium(speeds, macro, heat):
    density = macro[0]
    vel_x = macro[1] / density
    vel_y = macro[2] / density
    vel_z = macro[3] / density
    temper = (
        2.0 / 3.0 * (macro[4] / density - 0.5 * (vel_x * vel_x + vel_y * vel_y + vel_z * vel_z))
    )
    rel_x = speeds[0][:, None, None] - vel_x[None]
    rel_y = speeds[1][:, None, None] - vel_y[None]
    rel_z = speeds[2][:, None, None] - vel_z[None]
    rel_sq = rel_x * rel_x + rel_y * rel_y + rel_z * rel_z
    along = rel_x * heat[0][None] + rel_y * heat[1][None] + rel_z * heat[2][None]
    shakhov = 1.0 + (1.0 - PRANDTL) * along * (rel_sq / temper - 5.0) / (
        5.0 * density * temper * temper
    )
    return density * temper ** (-1.5) * jnp.exp(-rel_sq / (2.0 * temper)) * shakhov


def relax_rate(macro):
    density = macro[0]
    vel_x = macro[1] / density
    vel_y = macro[2] / density
    vel_z = macro[3] / density
    temper = (
        2.0 / 3.0 * (macro[4] / density - 0.5 * (vel_x * vel_x + vel_y * vel_y + vel_z * vel_z))
    )
    return KINETIC_STEP * density * temper ** (1.0 - VISCOSITY_POWER) / VISCOSITY_REF


def warming(center, minus_one, minus_two, plus_one, plus_two, courant):
    ahead = jnp.maximum(courant, 0.0)
    behind = jnp.maximum(-courant, 0.0)
    return (
        ahead * 0.5 * (3.0 * center - 4.0 * minus_one + minus_two)
        - ahead * ahead * 0.5 * (center - 2.0 * minus_one + minus_two)
        + behind * 0.5 * (3.0 * center - 4.0 * plus_one + plus_two)
        - behind * behind * 0.5 * (center - 2.0 * plus_one + plus_two)
    )


def kinetic(padded, speeds, feq, rate, inflow_dist, inflow_mask):
    center = padded[:, 2:-2]
    adv_x = warming(
        center,
        padded[:, 1:-3],
        padded[:, :-4],
        padded[:, 3:-1],
        padded[:, 4:],
        KINETIC_STEP * speeds[0][:, None, None],
    )
    adv_y = warming(
        center,
        jnp.roll(center, NZ, axis=-1),
        jnp.roll(center, 2 * NZ, axis=-1),
        jnp.roll(center, -NZ, axis=-1),
        jnp.roll(center, -2 * NZ, axis=-1),
        KINETIC_STEP * speeds[1][:, None, None],
    )
    back_one = roll_z(center, 1)
    front_one = roll_z(center, -1)
    adv_z = warming(
        center,
        back_one,
        roll_z(back_one, 1),
        front_one,
        roll_z(front_one, -1),
        KINETIC_STEP * speeds[2][:, None, None],
    )
    updated = center - (adv_x + adv_y + adv_z) + rate[None] * (feq - center)
    return jnp.where(inflow_mask[None] == 1, inflow_dist[:, None, None], updated)


def inflow_values(speeds, inflow_scalars, inflow_drift):
    rel_x = speeds[0] - inflow_drift[0]
    rel_y = speeds[1] - inflow_drift[1]
    rel_z = speeds[2] - inflow_drift[2]
    rel_sq = rel_x * rel_x + rel_y * rel_y + rel_z * rel_z
    return (
        inflow_scalars[0]
        * inflow_scalars[1] ** (-1.5)
        * jnp.exp(-rel_sq / (2.0 * inflow_scalars[1]))
    )


def fix_ends(padded, ghosts, space_index, space_count):
    first = jnp.broadcast_to(padded[:, ghosts : ghosts + 1], padded[:, :ghosts].shape)
    last = jnp.broadcast_to(padded[:, -ghosts - 1 : -ghosts], padded[:, -ghosts:].shape)
    lower = jnp.where(space_index == 0, first, padded[:, :ghosts])
    upper = jnp.where(space_index == space_count - 1, last, padded[:, -ghosts:])
    return jnp.concatenate([lower, padded[:, ghosts:-ghosts], upper], axis=1)


def solve_macro(fields, space_index, space_count):
    padded = extended(fields, (("space", 1),), MSTEPS)
    padded = fix_ends(padded, MSTEPS, space_index, space_count)
    extra = padded[5:]
    state = padded[:5]
    total_planes = extra.shape[1]
    for substep in range(MSTEPS):
        if substep > 0:
            state = fix_ends(state, MSTEPS - substep, space_index, space_count)
        state = macro_step(state, extra[:, substep : total_planes - substep])
    return state


def per_device(distribution, block_map, inflow_mask, owner_map, inflow_scalars, inflow_drift):
    vel_count = lax.axis_size("vel")
    vel_index = lax.axis_index("vel")
    space_count = lax.axis_size("space")
    space_index = lax.axis_index("space")
    local_vel, planes, width = distribution.shape
    cells = planes * width
    block_len = cells // vel_count
    node_ids = (block_map[:, None] * VB + jnp.arange(VB, dtype=jnp.int32)[None, :]).reshape(-1)
    speeds = coordinates(node_ids)
    rows = moment_rows(*speeds)
    inflow_dist = inflow_values(speeds, inflow_scalars, inflow_drift)
    current = distribution
    macro = None
    partial_sum = jnp.dot(rows, current.reshape(local_vel, cells), precision=HIGHEST)
    rimmed = extended(current, (("space", 1),), 2)
    total = lax.psum(partial_sum, "vel")
    fields = convert(total).reshape(13, planes, width)
    macro = solve_macro(fields, space_index, space_count)
    heat = fields[10:13]
    rate = relax_rate(macro)
    feq = equilibrium(speeds, macro, heat)
    lower = jnp.where(
        space_index == 0,
        jnp.broadcast_to(inflow_dist[:, None, None], (local_vel, 2, width)),
        rimmed[:, :2],
    )
    upper = jnp.where(
        space_index == space_count - 1,
        jnp.broadcast_to(rimmed[:, -3:-2], (local_vel, 2, width)),
        rimmed[:, -2:],
    )
    padded = jnp.concatenate([lower, rimmed[:, 2:-2], upper], axis=1)
    current = kinetic(padded, speeds, feq, rate, inflow_dist, inflow_mask)
    blocks = macro.reshape(5, vel_count, block_len)
    mine = lax.dynamic_slice_in_dim(blocks, owner_map[vel_index], 1, axis=1).reshape(5, block_len)
    return (current, mine)


def solution(mesh):
    return jax.shard_map(
        per_device,
        mesh=mesh,
        in_specs=(P("vel", "space", None), P("vel"), P("space", None), P(), P(), P()),
        out_specs=(P("vel", "space", None), P(None, ("space", "vel"))),
        check_vma=False,
    )
```

profile of v0, /device:TPU:1, one launch (start us, length us, event | category | flops | bytes accessed | tf_op | source)
XLA Modules:
  0.0 361.7 jit_solution(9289805104260025805)
XLA Ops:
  1.5 8.9 %copy.27 = f32[256,8,4,256]{3,1,2,0:T(8,128)} copy(f32[256,8,4,256]{3,2,1,0:T(4,128)} %bitcast.104) | data formatting | bytes 16777216
  10.6 6.4 %fusion.27 = f32[13,1024]{1,0:T(8,128)S(1)} fusion(f32[2048,1024]{1,0:T(8,128)} %bitcast.115, f32[13,2048]{1,0:T(8,128)S(1)} %stack.49), kind=kOutput, calls=%fused_computation.126 | convolution fusion | flops 327182336 | bytes 8548352 | tf_op jit(solution)/shard_map/dot_general | solution.py:325
  17.0 31.4 %psum.7 = f32[13,1024]{1,0:T(8,128)S(1)} all-reduce(f32[13,1024]{1,0:T(8,128)S(1)} %fusion.27), channel_id=1, replica_groups=mesh['vel'=8,'space'=4] {'vel'}, use_global_device_ids=true, to_apply=%region_0.1 | all-reduce | flops 13312 | bytes 106496 | tf_op jit(solution)/shard_map/psum | solution.py:327
  51.4 10.9 %collective-permute-start.2 = (f32[13,4,256]{2,1,0:T(4,128)S(1)}, f32[13,4,256]{2,1,0:T(4,128)S(1)}, u32[]{:S(2)}, u32[]{:S(2)}) collective-permute-start(f32[13,4,256]{2,1,0:T(4,128)S(1)} %constant_dynamic-update-slice_fusion), channel_id=1, source_target_pairs={{0,1},{1,2},{2,3},{4,5},{5,6},{6,7},{8,9},{9,10},{10,11},{12,13},{... | collective-permute-start | bytes 159752 | tf_op jit(solution)/shard_map/ppermute | solution.py:33
  64.3 9.0 %fusion.162 = (f32[2048,2,256]{2,1,0:T(2,128)S(1)}, f32[2048,2,256]{2,1,0:T(2,128)S(1)}) fusion(f32[2048,4,256]{2,1,0:T(4,128)} %param.6), kind=kLoop, calls=%fused_computation.438 | loop fusion | bytes 16777216 | tf_op jit(solution)/shard_map/slice | solution.py:31
  75.7 3.8 %collective-permute-start = (f32[2048,2,256]{2,0,1:T(8,128)}, f32[2048,2,256]{2,0,1:T(8,128)}, u32[]{:S(2)}, u32[]{:S(2)}) collective-permute-start(f32[2048,2,256]{2,0,1:T(8,128)} %copy.23), channel_id=1, source_target_pairs={{0,1},{1,2},{2,3},{4,5},{5,6},{6,7},{8,9},{9,10},{10,11},{12,13},{... | collective-permute-start | bytes 12582920 | tf_op jit(solution)/shard_map/ppermute | solution.py:33
  82.0 2.8 collective-permute-start.1
  85.0 8.5 %fusion.168 = (f32[2048,4,255]{2,1,0:T(4,128)}, f32[2048,4,255]{2,1,0:T(4,128)}) fusion(f32[2048,4,256]{2,1,0:T(4,128)S(1)} %bitcast.106), kind=kLoop, calls=%fused_computation.444 | loop fusion | bytes 33423360 | tf_op jit(solution)/shard_map/jit(_roll_static)/slice | solution.py:140
  93.5 8.2 %fusion.169 = (f32[2048,4,241]{2,1,0:T(4,128)}, f32[2048,4,241]{2,1,0:T(4,128)}) fusion(f32[2048,4,256]{2,1,0:T(4,128)S(1)} %bitcast.106), kind=kLoop, calls=%fused_computation.445 | loop fusion | bytes 31588352 | tf_op jit(solution)/shard_map/jit(_roll_static)/slice | solution.py:140
  101.7 4.2 %fusion.167 = (f32[2048,4,1]{2,1,0:T(4,128)S(1)}, f32[2048,4,1]{2,1,0:T(4,128)}) fusion(f32[2048,4,256]{2,1,0:T(4,128)S(1)} %bitcast.106), kind=kLoop, calls=%fused_computation.443 | loop fusion | bytes 131072 | tf_op jit(solution)/shard_map/jit(_roll_static)/slice | solution.py:140
  105.8 4.9 %fusion.170 = (f32[2048,4,15]{2,1,0:T(4,128)}, f32[2048,4,15]{2,1,0:T(4,128)}) fusion(f32[2048,4,256]{2,1,0:T(4,128)S(1)} %bitcast.106), kind=kLoop, calls=%fused_computation.446 | loop fusion | bytes 1966080 | tf_op jit(solution)/shard_map/jit(_roll_static)/slice | solution.py:140
  110.7 8.4 %fusion.164 = (f32[2048,4,240]{2,1,0:T(4,128)}, f32[2048,4,240]{2,1,0:T(4,128)}) fusion(f32[2048,4,256]{2,1,0:T(4,128)S(1)} %bitcast.106), kind=kLoop, calls=%fused_computation.440 | loop fusion | bytes 31457280 | tf_op jit(solution)/shard_map/jit(_roll_static)/slice | solution.py:258
  119.1 8.3 %fusion.166 = (f32[2048,4,224]{2,1,0:T(4,128)}, f32[2048,4,224]{2,1,0:T(4,128)}) fusion(f32[2048,4,256]{2,1,0:T(4,128)S(1)} %bitcast.106), kind=kLoop, calls=%fused_computation.442 | loop fusion | bytes 29360128 | tf_op jit(solution)/shard_map/jit(_roll_static)/slice | solution.py:259
  127.4 4.9 %fusion.163 = (f32[2048,4,16]{2,1,0:T(4,128)}, f32[2048,4,16]{2,1,0:T(4,128)}) fusion(f32[2048,4,256]{2,1,0:T(4,128)S(1)} %bitcast.106), kind=kLoop, calls=%fused_computation.439 | loop fusion | bytes 2097152 | tf_op jit(solution)/shard_map/jit(_roll_static)/slice | solution.py:258
  132.2 5.1 %fusion.165 = (f32[2048,4,32]{2,1,0:T(4,128)}, f32[2048,4,32]{2,1,0:T(4,128)}) fusion(f32[2048,4,256]{2,1,0:T(4,128)S(1)} %bitcast.106), kind=kLoop, calls=%fused_computation.441 | loop fusion | bytes 4194304 | tf_op jit(solution)/shard_map/jit(_roll_static)/slice | solution.py:259
  142.6 25.2 %maximum_select_fusion = (f32[2048,4,256]{2,1,0:T(4,128)}, f32[2048,4,256]{2,1,0:T(4,128)}) fusion(f32[2048,4,15]{2,1,0:T(4,128)} %get-tuple-element.66, f32[2048,4,241]{2,1,0:T(4,128)} %get-tuple-element.64, f32[2048,4,255]{2,1,0:T(4,128)} %get-tuple-element.62, f32[2048,4,1]{2,1,0:T(4,128)S(1)} %get-tuple-element.60, ...), kind=kLoop, calls=%fused_computation.28 | loop fusion | flops 12582912 | bytes 50332160 | tf_op jit(solution)/shard_map/jit(_where)/select_n | solution.py:139
  167.8 10.2 %slice.1200 = f32[2048,4,241]{2,1,0:T(4,128)} slice(f32[2048,4,256]{2,1,0:T(4,128)} %get-tuple-element.264), slice={[0:2048], [0:4], [15:256]} | slice | bytes 15794176 | tf_op jit(solution)/shard_map/jit(_roll_static)/slice | solution.py:140
  180.5 3.6 slice.1202
  184.2 6.1 %slice.1206 = f32[2048,4,255]{2,1,0:T(4,128)} slice(f32[2048,4,256]{2,1,0:T(4,128)S(1)} %bitcast.114), slice={[0:2048], [0:4], [1:256]} | slice | bytes 16711680 | tf_op jit(solution)/shard_map/jit(_roll_static)/slice | solution.py:143
  190.2 3.6 %slice.1204 = f32[2048,4,15]{2,1,0:T(4,128)} slice(f32[2048,4,256]{2,1,0:T(4,128)S(1)} %bitcast.114), slice={[0:2048], [0:4], [241:256]} | slice | bytes 983040 | tf_op jit(solution)/shard_map/jit(_roll_static)/slice | solution.py:143
  212.1 12.2 %copy.12 = f32[2048,2,256]{2,1,0:T(2,128)} copy(f32[2048,2,256]{2,0,1:T(8,128)S(1)} %broadcast_select_fusion.1) | data formatting | bytes 8388608 | tf_op jit(solution)/shard_map/jit(_where)/select_n | solution.py:333
  224.4 2.8 broadcast_select_fusion
  227.2 12.2 %copy.15 = f32[2048,2,256]{2,1,0:T(2,128)} copy(f32[2048,2,256]{2,0,1:T(8,128)S(1)} %broadcast_select_fusion) | data formatting | bytes 8388608 | tf_op jit(solution)/shard_map/jit(_where)/select_n | solution.py:338
  239.5 121.7 %add_select_fusion = f32[2048,4,256]{2,1,0:T(4,128)} fusion(f32[2048,4,256]{2,1,0:T(4,128)S(1)} %bitcast.108, f32[2048,4,256]{2,1,0:T(4,128)} %get-tuple-element.265, f32[2048,4,1]{2,1,0:T(4,128)} %slice.1207, f32[2048,4,255]{2,1,0:T(4,128)} %slice.1206, f32[2048,4,241]{2,1,0:T(4,128)} %bitcast.112, f32[2048,4,15]{2,1,0:T(4,128)} %slice.1204, ...), kind=kLoop, calls=%fused_computation.32 | loop fusion | flops 213909504 | bytes 109229568 | tf_op jit(solution)/shard_map/jit(_where)/select_n | solution.py:275
  (198 shorter events, 32.4 us)
Async XLA Ops:
  51.4 151.4 %collective-permute-start.2 = (f32[13,4,256]{2,1,0:T(4,128)S(1)}, f32[13,4,256]{2,1,0:T(4,128)S(1)}, u32[]{:S(2)}, u32[]{:S(2)}) collective-permute-start(f32[13,4,256]{2,1,0:T(4,128)S(1)} %constant_dynamic-update-slice_fusion), channel_id=1, source_target_pairs={{0,1},{1,2},{2,3},{4,5},{5,6},{6,7},{8,9},{9,10},{10,11},{12,13},{... | collective-permute-start | bytes 159752 | tf_op jit(solution)/shard_map/ppermute | solution.py:33
  62.3 140.5 %collective-permute-start.3 = (f32[13,4,256]{2,1,0:T(4,128)S(1)}, f32[13,4,256]{2,1,0:T(4,128)S(1)}, u32[]{:S(2)}, u32[]{:S(2)}) collective-permute-start(f32[13,4,256]{2,1,0:T(4,128)S(1)} %constant_dynamic-update-slice_fusion), channel_id=1, source_target_pairs={{1,0},{2,1},{3,2},{5,4},{6,5},{7,6},{9,8},{10,9},{11,10},{13,12},{... | collective-permute-start | bytes 159752 | tf_op jit(solution)/shard_map/ppermute | solution.py:34
  73.3 11.7 %slice-start = ((s8[8388608]{0:T(1024)(128)(4,1)}), s8[4194304]{0:T(1024)(128)(4,1)S(1)}, s32[]{:S(2)}) async-start(s8[8388608]{0:T(1024)(128)(4,1)} %bitcast.105), calls=%async_computation | async-start | bytes 8388608
  75.7 133.7 %collective-permute-start = (f32[2048,2,256]{2,0,1:T(8,128)}, f32[2048,2,256]{2,0,1:T(8,128)}, u32[]{:S(2)}, u32[]{:S(2)}) collective-permute-start(f32[2048,2,256]{2,0,1:T(8,128)} %copy.23), channel_id=1, source_target_pairs={{0,1},{1,2},{2,3},{4,5},{5,6},{6,7},{8,9},{9,10},{10,11},{12,13},{... | collective-permute-start | bytes 12582920 | tf_op jit(solution)/shard_map/ppermute | solution.py:33
  79.5 5.4 %slice-start.1 = ((s8[8388608]{0:T(1024)(128)(4,1)}), s8[4194304]{0:T(1024)(128)(4,1)S(1)}, s32[]{:S(2)}) async-start(s8[8388608]{0:T(1024)(128)(4,1)} %bitcast.105), calls=%async_computation.1 | async-start | bytes 8388608
  82.0 142.3 %collective-permute-start.1 = (f32[2048,2,256]{2,0,1:T(8,128)}, f32[2048,2,256]{2,0,1:T(8,128)}, u32[]{:S(2)}, u32[]{:S(2)}) collective-permute-start(f32[2048,2,256]{2,0,1:T(8,128)} %copy.25), channel_id=1, source_target_pairs={{1,0},{2,1},{3,2},{5,4},{6,5},{7,6},{9,8},{10,9},{11,10},{13,12},{... | collective-permute-start | bytes 12582920 | tf_op jit(solution)/shard_map/ppermute | solution.py:34
  132.2 5.1 %copy-start.6 = (f32[2]{0:T(128)S(1)}, f32[2]{0:T(128)}, u32[]{:S(2)}) copy-start(f32[2]{0:T(128)} %param.10) | copy-start | bytes 28
  132.2 5.8 %copy-start.4 = (f32[3]{0:T(128)S(1)}, f32[3]{0:T(128)}, u32[]{:S(2)}) copy-start(f32[3]{0:T(128)} %param.11) | copy-start | bytes 40
  142.6 25.2 %copy-start.5 = (s32[4,256]{1,0:T(4,128)S(1)}, s32[4,256]{1,0:T(4,128)}, u32[]{:S(2)}) copy-start(s32[4,256]{1,0:T(4,128)} %param.8) | copy-start | bytes 12292
  167.8 10.2 %copy-start = (f32[2048,4,256]{2,1,0:T(4,128)S(1)}, f32[2048,4,256]{2,1,0:T(4,128)}, u32[]{:S(2)}) copy-start(f32[2048,4,256]{2,1,0:T(4,128)} %get-tuple-element.264) | copy-start | bytes 25165828
  178.0 6.1 %slice-start.6 = ((s8[8388608]{0:T(1024)(128)(4,1)}), s8[4194304]{0:T(1024)(128)(4,1)S(1)}, s32[]{:S(2)}) async-start(s8[8388608]{0:T(1024)(128)(4,1)} %bitcast.113), calls=%async_computation.6 | async-start | bytes 8388608
  180.5 3.6 %slice-start.7 = ((s8[8388608]{0:T(1024)(128)(4,1)}), s8[4194304]{0:T(1024)(128)(4,1)S(1)}, s32[]{:S(2)}) async-start(s8[8388608]{0:T(1024)(128)(4,1)} %bitcast.113), calls=%async_computation.7 | async-start | bytes 8388608
  193.9 4.9 %copy-start.7 = (s32[8]{0:T(128)S(1)}, s32[8]{0:T(128)}, u32[]{:S(2)}) copy-start(s32[8]{0:T(128)} %param.9) | copy-start | bytes 100
  209.4 14.9 %copy-start.3 = (f32[2048,1,256]{2,0,1:T(8,128)S(1)}, f32[2048,1,256]{2,0,1:T(8,128)}, u32[]{:S(2)}) copy-start(f32[2048,1,256]{2,0,1:T(8,128)} %copy.36) | copy-start | bytes 6291460
  212.1 27.3 %slice-start.4 = ((s8[8388608]{0:T(1024)(128)(4,1)}), s8[4194304]{0:T(1024)(128)(4,1)S(1)}, s32[]{:S(2)}) async-start(s8[8388608]{0:T(1024)(128)(4,1)} %bitcast.109), calls=%async_computation.4 | async-start | bytes 8388608
  212.1 27.3 %copy-start.2 = (f32[2048,4,1]{2,1,0:T(4,128)S(1)}, f32[2048,4,1]{2,1,0:T(4,128)}, u32[]{:S(2)}) copy-start(f32[2048,4,1]{2,1,0:T(4,128)} %slice.1202) | copy-start | bytes 98308
  224.3 15.1 %slice-start.2 = ((s8[8388608]{0:T(1024)(128)(4,1)}), s8[4194304]{0:T(1024)(128)(4,1)S(1)}, s32[]{:S(2)}) async-start(s8[8388608]{0:T(1024)(128)(4,1)} %bitcast.107), calls=%async_computation.2 | async-start | bytes 8388608
  224.4 15.1 %slice-start.3 = ((s8[8388608]{0:T(1024)(128)(4,1)}), s8[4194304]{0:T(1024)(128)(4,1)S(1)}, s32[]{:S(2)}) async-start(s8[8388608]{0:T(1024)(128)(4,1)} %bitcast.107), calls=%async_computation.3 | async-start | bytes 8388608
  224.4 15.1 %slice-start.5 = ((s8[8388608]{0:T(1024)(128)(4,1)}), s8[4194304]{0:T(1024)(128)(4,1)S(1)}, s32[]{:S(2)}) async-start(s8[8388608]{0:T(1024)(128)(4,1)} %bitcast.109), calls=%async_computation.5 | async-start | bytes 8388608
  224.4 15.1 %copy-start.1 = (f32[2048,4,15]{2,1,0:T(4,128)S(1)}, f32[2048,4,15]{2,1,0:T(4,128)}, u32[]{:S(2)}) copy-start(f32[2048,4,15]{2,1,0:T(4,128)} %slice.1201) | copy-start | bytes 1474564
where the time goes:
time: 367 us; the launch traced here: 362 us
  other arithmetic  159 us (43%)
  local copies, waits for them, and re-layouts  139 us (38%)
  blocking collectives  31.4 us (9%)
  starting transfers between devices  19.4 us (5%)
  matrix products  6.4 us (2%)
  between operations  6.03 us (2%)
    select_n x1, other arithmetic, kinetic(): jnp.where(inflow_mask[None] == 1, inflow_dist[:, None, None], updated)  122 us
    psum x1, blocking collectives, per_device(): total = lax.psum(partial_sum, 'vel')  31.4 us
    slice x12, local copies, waits for them, and re-layouts, roll_z(): jnp.roll(values, 1 - NZ, axis=-1)  26.4 us
    select_n x1, other arithmetic, roll_z(): jnp.where(position == 0, jnp.roll(values, 1 - NZ, axis=-1), jnp.roll(valu...  25.2 us
    slice x11, local copies, waits for them, and re-layouts, roll_z(): jnp.roll(values, 1, axis=-1)  16.9 us
    unnamed x56, local copies, waits for them, and re-layouts  16 us
    ppermute x2, starting transfers between devices, extended(): before = lax.ppermute(last, axis, up)  14.7 us
    slice x2, local copies, waits for them, and re-layouts, kinetic(): jnp.roll(center, 2 * NZ, axis=-1)  13.4 us
  transfers between devices with their start and end apart: 4, of which 0 were waited for; matrix products, arithmetic and copies ran while one was open for 41% of the time, Pallas kernels for 0%

commit v1 on v0

v1 whole, which is shorter than its diff:
```python
import functools
import math

import jax
import jax.numpy as jnp
from jax import lax
from jax.experimental import pallas as pl
from jax.experimental.pallas import tpu as pltpu
from jax.sharding import PartitionSpec as P

NVX = 32
NVY = 32
NVZ = 16
VB = 128
NZ = 16
MSTEPS = 4

SPEED_LIMIT = 3.5
KINETIC_STEP = 0.12
VISCOSITY_REF = 0.25
VISCOSITY_POWER = 0.81
MACRO_STEP = 0.1
DIFFUSION = 1.6

DX = 2.0 * SPEED_LIMIT / NVX
DY = 2.0 * SPEED_LIMIT / NVY
DZ = 2.0 * SPEED_LIMIT / NVZ
WEIGHT = DX * DY * DZ / (2.0 * math.pi) ** 1.5
ROWS = VB // NVZ
PARTS = NVY // ROWS
SUB = 8
LANES = 128
VMEM_LIMIT = 60 << 20
AHEAD = 4


def speed(index, spacing):
    return -SPEED_LIMIT + (index + 0.5) * spacing


def upwind(courant):
    return 1.5 * courant - 0.5 * courant * courant, courant * courant - 2.0 * courant, 0.5 * courant - 0.5 * courant * courant


def slot_sizes(blocks):
    first = max(1, blocks // 2)
    second = min(blocks // 4, blocks - first)
    return first, second, blocks - first - second


def block_speeds(block):
    along_x = (block // PARTS).astype(jnp.float32)
    base_y = ((block % PARTS) * ROWS).astype(jnp.float32)
    return speed(along_x, DX), speed(base_y, DY)


def sublane(shift):
    return lambda x: pltpu.roll(x, shift % SUB, 0)


def lane(shift):
    return lambda x: pltpu.roll(x, shift % LANES, 1)


def places():
    plane = lax.broadcasted_iota(jnp.int32, (SUB, LANES), 0) % 4
    spot = lax.broadcasted_iota(jnp.int32, (SUB, LANES), 1)
    return plane, spot, spot % NZ


def gather_kernel(sizes, bm_ref, f_hbm, mom_ref, *refs):
    kinds = sum(1 for s in sizes if s)
    up = refs[:kinds]
    down = refs[kinds:2 * kinds]
    fbuf, pack, acc, in_sem, out_sem = refs[2 * kinds:]
    blocks = bm_ref.shape[0]
    plane, _, _ = places()
    high = plane >= 2
    half = PARTS * NVX // 2
    offsets = [0]
    for s in sizes[:kinds]:
        offsets.append(offsets[-1] + s)

    def fetch(i):
        return pltpu.make_async_copy(f_hbm.at[pl.ds(i * VB, VB)], fbuf.at[pl.ds(i * VB, VB)], in_sem.at[i])

    for i in range(min(AHEAD, blocks)):
        fetch(i).start()
    for r in range(13):
        acc[r] = jnp.zeros((SUB, LANES), jnp.float32)

    def step(i, positives):
        @pl.when(i + AHEAD < blocks)
        def _():
            fetch(i + AHEAD).start()
        fetch(i).wait()
        block = bm_ref[i]
        positive = block >= half
        cx, cy0 = block_speeds(block)

        def row(upward):
            def body(y, carry):
                cy = cy0 + y.astype(jnp.float32) * DY
                s0 = s1 = s2 = s3 = None
                for e in range(NVZ // 2):
                    a = fbuf[i * VB + y * NVZ + e]
                    b = fbuf[i * VB + y * NVZ + e + NVZ // 2]
                    if upward:
                        pack[i * (VB // 2) + y * (NVZ // 2) + e] = jnp.where(high, sublane(4)(a), sublane(2)(b))
                    else:
                        pack[i * (VB // 2) + y * (NVZ // 2) + e] = jnp.where(high, sublane(6)(b), sublane(4)(a))
                for e in range(NVZ // 2, NVZ):
                    z = speed(e, DZ)
                    a = fbuf[i * VB + y * NVZ + e]
                    b = fbuf[i * VB + y * NVZ + NVZ - 1 - e]
                    p = a + b
                    m = (a - b) * z
                    if s0 is None:
                        s0, s1, s2, s3 = p, m, p * (z * z), m * (z * z)
                    else:
                        s0, s1, s2, s3 = s0 + p, s1 + m, s2 + p * (z * z), s3 + m * (z * z)
                a0, a1, a2, a3, b0, b1, b2, c0, c1, d0 = carry
                t1 = s0 * cy
                t2 = t1 * cy
                u1 = s1 * cy
                return (a0 + s0, a1 + t1, a2 + t2, a3 + t2 * cy, b0 + s1, b1 + u1, b2 + u1 * cy, c0 + s2, c1 + s2 * cy, d0 + s3)

            zero = jnp.zeros((SUB, LANES), jnp.float32)
            a0, a1, a2, a3, b0, b1, b2, c0, c1, d0 = lax.fori_loop(0, ROWS, body, (zero,) * 10)
            x0 = a0 * cx
            xx = x0 * cx
            square = xx + a2 + c0
            terms = (a0, x0, a1, b0, square, xx, a2, a1 * cx, b0 * cx, b1, square * cx,
                     a1 * (cx * cx) + a3 + c1, b0 * (cx * cx) + b2 + d0)
            for r, term in enumerate(terms):
                acc[r] = acc[r] + term

        rank = jnp.where(positive, positives, i - positives)
        for upward in (True, False):
            @pl.when(positive if upward else jnp.logical_not(positive))
            def _(upward=upward):
                row(upward)
                for kind in range(kinds):
                    @pl.when(jnp.logical_and(rank >= offsets[kind], rank < offsets[kind + 1]))
                    def _(kind=kind):
                        target = (up if upward else down)[kind]
                        pltpu.make_async_copy(pack.at[pl.ds(i * (VB // 2), VB // 2)],
                                              target.at[pl.ds((rank - offsets[kind]) * (VB // 2), VB // 2)],
                                              out_sem.at[i]).start()
        return positives + jnp.where(positive, 1, 0)

    positives = lax.fori_loop(0, blocks, step, jnp.int32(0))
    for r in range(13):
        mom_ref[r] = acc[r] * WEIGHT
    limit = sizes[0] + sizes[1]
    excess = jnp.where(jnp.maximum(positives, blocks - positives) > limit, 1.0, 0.0)
    mom_ref[13] = jnp.full((SUB, LANES), excess, jnp.float32)

    def drain(i, carry):
        pltpu.make_async_copy(pack.at[pl.ds(i * (VB // 2), VB // 2)], up[0].at[pl.ds(0, VB // 2)], out_sem.at[i]).wait()
        return carry

    lax.fori_loop(0, blocks, drain, 0)


def gather(f, block_map, sizes):
    blocks = block_map.shape[0]
    half = VB // 2
    bufs = [jax.ShapeDtypeStruct((s * half, SUB, LANES), jnp.float32) for s in sizes if s]
    outs = pl.pallas_call(
        functools.partial(gather_kernel, sizes),
        in_specs=[pl.BlockSpec(memory_space=pltpu.SMEM), pl.BlockSpec(memory_space=pl.ANY)],
        out_specs=[pl.BlockSpec(memory_space=pltpu.VMEM)] + [pl.BlockSpec(memory_space=pl.ANY)] * (2 * len(bufs)),
        out_shape=[jax.ShapeDtypeStruct((14, SUB, LANES), jnp.float32)] + bufs + bufs,
        scratch_shapes=[pltpu.VMEM((blocks * VB, SUB, LANES), jnp.float32),
                        pltpu.VMEM((blocks * half, SUB, LANES), jnp.float32),
                        pltpu.VMEM((13, SUB, LANES), jnp.float32),
                        pltpu.SemaphoreType.DMA((blocks,)), pltpu.SemaphoreType.DMA((blocks,))],
        compiler_params=pltpu.CompilerParams(vmem_limit_bytes=VMEM_LIMIT),
        name="gather",
    )(block_map, f)
    n = len(bufs)
    return outs[0], outs[1:1 + n], outs[1 + n:]


def convert(m):
    inv = 1.0 / m[0]
    ux, uy, uz = m[1] * inv, m[2] * inv, m[3] * inv
    sq = ux * ux + uy * uy + uz * uz
    density = m[0]
    pressure = density * ((m[4] * inv - sq) / 3.0)
    xx, yy, xy, xz, yz = m[5:10]
    zz = m[4] - xx - yy
    sxx = xx - density * ux * ux - pressure
    syy = yy - density * uy * uy - pressure
    sxy = xy - density * ux * uy
    sxz = xz - density * ux * uz
    syz = yz - density * uy * uz
    hx = 0.5 * (m[10] - 2.0 * (ux * xx + uy * xy + uz * xz) - ux * m[4] + 2.0 * density * ux * sq)
    hy = 0.5 * (m[11] - 2.0 * (ux * xy + uy * yy + uz * yz) - uy * m[4] + 2.0 * density * uy * sq)
    hz = 0.5 * (m[12] - 2.0 * (ux * xz + uy * yz + uz * zz) - uz * m[4] + 2.0 * density * uz * sq)
    return [density, m[1], m[2], m[3], 0.5 * m[4]], [sxx, syy, sxy, sxz, syz, hx, hy, hz]


def primitive(state):
    density = state[0]
    inv = 1.0 / density
    ux, uy, uz = state[1] * inv, state[2] * inv, state[3] * inv
    temper = (2.0 / 3.0) * (state[4] * inv - 0.5 * (ux * ux + uy * uy + uz * uz))
    return density, ux, uy, uz, temper


def fluxes(state, extra):
    density, ux, uy, uz, temper = primitive(state)
    pressure = density * temper
    sxx, syy, sxy, sxz, syz, hx, hy, hz = extra
    szz = -sxx - syy
    enthalpy = state[4] + pressure
    fx = [state[1], state[1] * ux + pressure + sxx, state[2] * ux + sxy, state[3] * ux + sxz,
          enthalpy * ux + sxx * ux + sxy * uy + sxz * uz + hx]
    fy = [state[2], state[1] * uy + sxy, state[2] * uy + pressure + syy, state[3] * uy + syz,
          enthalpy * uy + sxy * ux + syy * uy + syz * uz + hy]
    fz = [state[3], state[1] * uz + sxz, state[2] * uz + syz, state[3] * uz + pressure + szz,
          enthalpy * uz + sxz * ux + syz * uy + szz * uz + hz]
    return fx, fy, fz


def macro_kernel(low_ref, own_ref, high_ref, macro_ref, cell_ref):
    plane, spot, along_z = places()
    index = lax.axis_index("space")
    count = lax.axis_size("space")
    first = (plane + index) == 0
    last = (plane + (count - 1 - index)) == 3
    last = jnp.logical_and(last, plane == 3)
    states, extras = [], []
    for ref in (low_ref, own_ref, high_ref):
        state, extra = convert([ref[r] for r in range(13)])
        states.append(state)
        extras.append(extra)

    def from_below(slabs):
        low, own, high = slabs
        a = sublane(1)(low)
        b = sublane(1)(jnp.where(plane == 3, sublane(4)(low), own))
        c = sublane(1)(jnp.where(plane == 3, sublane(4)(own), high))
        return [a, jnp.where(first, own, b), c]

    def from_above(slabs):
        low, own, high = slabs
        a = sublane(-1)(jnp.where(plane == 0, sublane(4)(own), low))
        b = sublane(-1)(jnp.where(plane == 0, sublane(4)(high), own))
        c = sublane(-1)(high)
        return [a, jnp.where(last, own, b), c]

    def y_minus(x):
        return lane(NZ)(jnp.where(spot >= LANES - NZ, sublane(4)(x), x))

    def y_plus(x):
        return lane(-NZ)(jnp.where(spot < NZ, sublane(4)(x), x))

    def z_minus(x):
        return lane(1)(jnp.where(along_z == NZ - 1, lane(-NZ)(x), x))

    def z_plus(x):
        return lane(-1)(jnp.where(along_z == 0, lane(NZ)(x), x))

    mix = DIFFUSION * MACRO_STEP
    push = 0.5 * MACRO_STEP
    for _ in range(MSTEPS):
        flux = [fluxes(s, e) for s, e in zip(states, extras)]
        fresh = [[], [], []]
        for r in range(5):
            scaled = [mix * states[k][r] for k in range(3)]
            xp = from_above([scaled[k] - push * flux[k][0][r] for k in range(3)])
            xm = from_below([scaled[k] + push * flux[k][0][r] for k in range(3)])
            for k in range(3):
                gy = push * flux[k][1][r]
                gz = push * flux[k][2][r]
                total = (1.0 - 6.0 * mix) * states[k][r] + xp[k] + xm[k]
                total = total + (y_plus(scaled[k] - gy) + y_minus(scaled[k] + gy))
                total = total + (z_plus(scaled[k] - gz) + z_minus(scaled[k] + gz))
                fresh[k].append(total)
        states = fresh
    state = states[1]
    for r in range(5):
        macro_ref[r] = state[r]
    density, ux, uy, uz, temper = primitive(state)
    logt = jnp.log(temper)
    rate = (KINETIC_STEP / VISCOSITY_REF) * density * jnp.exp((1.0 - VISCOSITY_POWER) * logt)
    skew = 1.0 / (15.0 * density * temper * temper)
    cell_ref[0] = ux
    cell_ref[1] = uy
    cell_ref[2] = uz
    cell_ref[3] = 0.5 / temper
    cell_ref[4] = rate * density * jnp.exp(-1.5 * logt)
    cell_ref[5] = extras[1][5] * skew
    cell_ref[6] = extras[1][6] * skew
    cell_ref[7] = extras[1][7] * skew
    cell_ref[8] = 1.0 - rate


def macro_solve(low, own, high):
    return pl.pallas_call(
        macro_kernel,
        out_shape=[jax.ShapeDtypeStruct((5, SUB, LANES), jnp.float32), jax.ShapeDtypeStruct((9, SUB, LANES), jnp.float32)],
        compiler_params=pltpu.CompilerParams(vmem_limit_bytes=VMEM_LIMIT),
        name="macro",
    )(low, own, high)


def kinetic_kernel(spans, aliased, bm_ref, scal_ref, drift_ref, mask_ref, cell_ref, f_hbm, *refs):
    kinds = len(spans)
    up = refs[:kinds]
    down = refs[kinds:2 * kinds]
    refs = refs[2 * kinds + (1 if aliased else 0):]
    out_hbm, fbuf, hbuf, gz_ref, az_ref, sz_ref, iz_ref, pick, in_sem, halo_sem, out_sem = refs
    blocks = bm_ref.shape[0]
    low_slot = spans[0][0]
    high_slot = spans[-1][1]
    half_id = PARTS * NVX // 2
    half = VB // 2
    index = lax.axis_index("space")
    count = lax.axis_size("space")

    def choose(i, carry):
        chosen, positives = carry
        positive = bm_ref[i] >= half_id
        rank = jnp.where(positive, positives, i - positives)
        take = jnp.logical_and(rank >= low_slot, rank < high_slot)

        @pl.when(take)
        def _():
            pick[0, chosen] = i
            pick[1, chosen] = rank
        return chosen + jnp.where(take, 1, 0), positives + jnp.where(positive, 1, 0)

    chosen, _ = lax.fori_loop(0, blocks, choose, (jnp.int32(0), jnp.int32(0)))

    def fetch(n):
        i = pick[0, n]
        return pltpu.make_async_copy(f_hbm.at[pl.ds(i * VB, VB)], fbuf.at[pl.ds(i * VB, VB)], in_sem.at[i])

    def begin(n):
        fetch(n).start()
        i = pick[0, n]
        rank = pick[1, n]
        positive = bm_ref[i] >= half_id
        for upward in (True, False):
            for kind, (lo, hi) in enumerate(spans):
                here = jnp.logical_and(rank >= lo, rank < hi)

                @pl.when(jnp.logical_and(here, positive if upward else jnp.logical_not(positive)))
                def _(upward=upward, kind=kind, lo=lo):
                    source = (up if upward else down)[kind]
                    pltpu.make_async_copy(source.at[pl.ds((rank - lo) * half, half)], hbuf.at[pl.ds(i * half, half)],
                                          halo_sem.at[i]).start()

    for n in range(min(AHEAD, blocks)):
        @pl.when(n < chosen)
        def _(n=n):
            begin(n)

    plane, spot, along_z = places()
    fixed = mask_ref[...] == 1
    ux, uy, uz, inv2t = cell_ref[0], cell_ref[1], cell_ref[2], cell_ref[3]
    hot = jnp.full((SUB, LANES), scal_ref[1], jnp.float32)
    hot_inv = 0.5 / hot
    hot_scale = scal_ref[0] * jnp.exp(-1.5 * jnp.log(hot))
    for e in range(NVZ):
        cz = speed(e, DZ)
        rel = cz - uz
        t = rel * rel * inv2t
        gz_ref[e] = jnp.exp(-t)
        sz_ref[e] = 2.0 * t
        az_ref[e] = rel * cell_ref[7]
        off = cz - drift_ref[2]
        iz_ref[e] = jnp.exp(-(off * off) * hot_inv)

    def run(n, carry):
        @pl.when(n + AHEAD < chosen)
        def _():
            begin(n + AHEAD)
        i = pick[0, n]
        block = bm_ref[i]
        positive = block >= half_id
        y_positive = (block % PARTS) >= PARTS // 2
        cx, cy0 = block_speeds(block)
        fetch(n).wait()
        pltpu.make_async_copy(up[0].at[pl.ds(0, half)], hbuf.at[pl.ds(i * half, half)], halo_sem.at[i]).wait()
        k0x, k1x, k2x = upwind(KINETIC_STEP * jnp.abs(cx))
        relx = cx - ux
        tx = relx * relx * inv2t
        ax = relx * cell_ref[5]
        offx = cx - drift_ref[0]

        def rows(x_up, edge, y_up):
            def body(y, carry):
                cy = cy0 + y.astype(jnp.float32) * DY
                k0y, k1y, k2y = upwind(KINETIC_STEP * jnp.abs(cy))
                rely = cy - uy
                txy = tx + rely * rely * inv2t
                axy = ax + rely * cell_ref[6]
                gxy = cell_ref[4] * jnp.exp(-txy)
                sxy = 2.0 * txy - 5.0
                keep = cell_ref[8] - (k0x + k0y)
                offy = cy - drift_ref[1]
                ixy = hot_scale * jnp.exp(-(offx * offx + offy * offy) * hot_inv)
                for e in range(NVZ):
                    k0z, k1z, k2z = upwind(KINETIC_STEP * abs(speed(e, DZ)))
                    spot_v = i * VB + y * NVZ + e
                    f = fbuf[spot_v]
                    inflow = ixy * iz_ref[e]
                    total = f * (keep - k0z)
                    if edge and x_up:
                        halo = inflow
                    elif not edge:
                        halo = hbuf[i * half + y * (NVZ // 2) + e % (NVZ // 2)]
                        if e >= NVZ // 2:
                            halo = sublane(2 if x_up else -2)(halo)
                    else:
                        halo = jnp.where(plane == 0, sublane(1)(f), sublane(2)(f))
                    if x_up:
                        x1 = sublane(1)(jnp.where(plane == 3, halo, f))
                        x2 = sublane(2)(jnp.where(plane >= 2, halo, f))
                    else:
                        x1 = sublane(-1)(jnp.where(plane == 0, halo, f))
                        x2 = sublane(-2)(jnp.where(plane < 2, halo, f))
                    total = total - k1x * x1 - k2x * x2
                    across = sublane(4)(f)
                    if y_up:
                        y1 = lane(NZ)(jnp.where(spot >= LANES - NZ, across, f))
                        y2 = lane(2 * NZ)(jnp.where(spot >= LANES - 2 * NZ, across, f))
                    else:
                        y1 = lane(-NZ)(jnp.where(spot < NZ, across, f))
                        y2 = lane(-2 * NZ)(jnp.where(spot < 2 * NZ, across, f))
                    total = total - k1y * y1 - k2y * y2
                    if e >= NVZ // 2:
                        wrap = lane(-NZ)(f)
                        z1 = lane(1)(jnp.where(along_z == NZ - 1, wrap, f))
                        z2 = lane(2)(jnp.where(along_z >= NZ - 2, wrap, f))
                    else:
                        wrap = lane(NZ)(f)
                        z1 = lane(-1)(jnp.where(along_z == 0, wrap, f))
                        z2 = lane(-2)(jnp.where(along_z < 2, wrap, f))
                    total = total - k1z * z1 - k2z * z2
                    shape = 1.0 + (axy + az_ref[e]) * (sxy + sz_ref[e])
                    total = total + (gxy * gz_ref[e]) * shape
                    fbuf[spot_v] = jnp.where(fixed, inflow, total)
                return carry

            lax.fori_loop(0, ROWS, body, 0)

        for x_up in (True, False):
            outer = (index == 0) if x_up else (index == count - 1)
            for edge in (True, False):
                for y_up in (True, False):
                    flag = jnp.logical_and(positive if x_up else jnp.logical_not(positive),
                                           outer if edge else jnp.logical_not(outer))
                    flag = jnp.logical_and(flag, y_positive if y_up else jnp.logical_not(y_positive))

                    @pl.when(flag)
                    def _(x_up=x_up, edge=edge, y_up=y_up):
                        rows(x_up, edge, y_up)
        pltpu.make_async_copy(fbuf.at[pl.ds(i * VB, VB)], out_hbm.at[pl.ds(i * VB, VB)], out_sem.at[i]).start()
        return carry

    lax.fori_loop(0, chosen, run, 0)

    def drain(n, carry):
        i = pick[0, n]
        pltpu.make_async_copy(fbuf.at[pl.ds(i * VB, VB)], out_hbm.at[pl.ds(i * VB, VB)], out_sem.at[i]).wait()
        return carry

    lax.fori_loop(0, chosen, drain, 0)


def kinetic(f, block_map, scalars, drift, mask, cells, spans, up, down, into=None):
    blocks = block_map.shape[0]
    half = VB // 2
    smem = pl.BlockSpec(memory_space=pltpu.SMEM)
    vmem = pl.BlockSpec(memory_space=pltpu.VMEM)
    hbm = pl.BlockSpec(memory_space=pl.ANY)
    operands = [block_map, scalars, drift, mask, cells, f, *up, *down]
    specs = [smem, smem, smem, vmem, vmem, hbm] + [hbm] * (len(up) + len(down))
    aliases = {}
    if into is not None:
        aliases = {len(operands): 0}
        operands.append(into)
        specs.append(hbm)
    table = pltpu.VMEM((NVZ, SUB, LANES), jnp.float32)
    return pl.pallas_call(
        functools.partial(kinetic_kernel, spans, into is not None),
        in_specs=specs,
        out_specs=hbm,
        out_shape=jax.ShapeDtypeStruct(f.shape, jnp.float32),
        scratch_shapes=[pltpu.VMEM((blocks * VB, SUB, LANES), jnp.float32), pltpu.VMEM((blocks * half, SUB, LANES), jnp.float32),
                        table, table, table, table, pltpu.SMEM((2, blocks), jnp.int32),
                        pltpu.SemaphoreType.DMA((blocks,)), pltpu.SemaphoreType.DMA((blocks,)), pltpu.SemaphoreType.DMA((blocks,))],
        input_output_aliases=aliases,
        compiler_params=pltpu.CompilerParams(vmem_limit_bytes=VMEM_LIMIT),
        name="kinetic",
    )(*operands)


def over_vel(values):
    count = lax.axis_size("vel")
    if count & (count - 1):
        return lax.psum(values, "vel")
    reach = 1
    while reach < count:
        values = values + lax.ppermute(values, "vel", [(i, i ^ reach) for i in range(count)])
        reach *= 2
    return values


def tiles(array):
    lead, planes, width = array.shape
    return array.reshape(lead, planes, width // LANES, LANES).transpose(0, 2, 1, 3).reshape(lead, planes * width // LANES, LANES)


def per_device(distribution, block_map, inflow_mask, owner_map, inflow_scalars, inflow_drift):
    vel_count = lax.axis_size("vel")
    vel_index = lax.axis_index("vel")
    space_count = lax.axis_size("space")
    local_vel, planes, width = distribution.shape
    assert planes == MSTEPS and planes * width == SUB * LANES
    block_len = planes * width // vel_count
    blocks = block_map.shape[0]
    sizes = slot_sizes(blocks)
    f = tiles(distribution)
    mask = tiles(inflow_mask[None])[0]
    rise = [(i, i + 1) for i in range(space_count - 1)]
    fall = [(i + 1, i) for i in range(space_count - 1)]

    partial, ups, downs = gather(f, block_map, sizes)
    got_up = [lax.ppermute(ups[0], "space", rise)]
    got_down = [lax.ppermute(downs[0], "space", fall)]
    if sizes[1]:
        got_up.append(lax.ppermute(ups[1], "space", rise))
        got_down.append(lax.ppermute(downs[1], "space", fall))
    total = over_vel(partial)
    low = lax.ppermute(total[:13], "space", rise)
    high = lax.ppermute(total[:13], "space", fall)
    macro, cells = macro_solve(low, total, high)
    common = (f, block_map, inflow_scalars, inflow_drift, mask, cells)
    updated = kinetic(*common, ((0, sizes[0]),), got_up[:1], got_down[:1])
    if sizes[1]:
        edge = sizes[0] + sizes[1]
        spans = ((sizes[0], edge),)
        if sizes[2]:
            spans = spans + ((edge, blocks),)
            extra = lax.cond(total[13, 0, 0] > 0.5,
                             lambda a, b: (lax.ppermute(a, "space", rise), lax.ppermute(b, "space", fall)),
                             lambda a, b: (a, b), ups[2], downs[2])
            got_up.append(extra[0])
            got_down.append(extra[1])
        updated = kinetic(*common, spans, got_up[1:], got_down[1:], into=updated)
    current = updated.reshape(local_vel, width // LANES, planes, LANES).transpose(0, 2, 1, 3).reshape(local_vel, planes, width)
    flat = macro.reshape(5, width // LANES, planes, LANES).transpose(0, 2, 1, 3).reshape(5, vel_count, block_len)
    mine = lax.dynamic_slice_in_dim(flat, owner_map[vel_index], 1, axis=1).reshape(5, block_len)
    return (current, mine)


def solution(mesh):
    return jax.shard_map(
        per_device,
        mesh=mesh,
        in_specs=(P("vel", "space", None), P("vel"), P("space", None), P(), P(), P()),
        out_specs=(P("vel", "space", None), P(None, ("space", "vel"))),
        check_vma=False,
    )
```

time: 367 us -> 95.4 us (0.26); the launches traced: 362 us -> 94.1 us
  other arithmetic: 159 us -> 0.85 us
  local copies, waits for them, and re-layouts: 139 us -> 5.45 us
  Pallas kernels: 0 us -> 40.7 us
  blocking collectives: 31.4 us -> 0 us
  waiting for transfers between devices: 0.01 us -> 20.3 us
  matrix products: 6.4 us -> 0 us
  starting transfers between devices: 19.4 us -> 23.4 us
    select_n x9 -> x0, other arithmetic: 152 us -> none  [the longest x1 122 us: kinetic(): jnp.where(inflow_mask[None] == 1, inflow_dist[:, None, None], updated)]
    slice x73 -> x2, local copies, waits for them, and re-layouts: 97.5 us -> 0.53 us  [the longest x1 0.52 us: per_device(): total[13, 0, 0] > 0.5]
    pallas_call x0 -> x4, Pallas kernels: none -> 40.7 us  [the longest x2 30.5 us: kinetic(): pl.pallas_call(functools.partial(kinetic_kernel, spans, into is not None)...]
    psum x1 -> x0, blocking collectives: 31.4 us -> none  [per_device(): total = lax.psum(partial_sum, 'vel')]
    select_n x2 -> x0, local copies, waits for them, and re-layouts: 24.5 us -> none  [the longest x1 12.2 us: per_device(): jnp.where(space_index == space_count - 1, jnp.broadcast_to(rimmed[:, -3:-...]
    ppermute x4 -> x9, waiting for transfers between devices: 0.01 us -> 20.3 us  [the longest x1 16.5 us: per_device(): high = lax.ppermute(total[:13], 'space', fall)]
    unnamed x56 -> x13, local copies, waits for them, and re-layouts: 16 us -> 3.59 us
    dot_general x1 -> x0, matrix products: 6.4 us -> none  [per_device(): jnp.dot(rows, current.reshape(local_vel, cells), precision=HIGHEST)]
  transfers between devices with their start and end apart: 4 -> 9, of which waited for: 0 -> 3; matrix products, arithmetic and copies ran while one was open for 41% -> 4% of each run, Pallas kernels for 0% -> 30%
where the time goes in v1:
time: 95.4 us; the launch traced here: 94.1 us
  Pallas kernels  40.7 us (43%)
  starting transfers between devices  23.4 us (25%)
  waiting for transfers between devices  20.3 us (21%)
  local copies, waits for them, and re-layouts  5.45 us (6%)
  between operations  3.43 us (4%)
    pallas_call x2, Pallas kernels, kinetic(): pl.pallas_call(functools.partial(kinetic_kernel, spans, into is not None)...  30.5 us
    ppermute x1, waiting for transfers between devices, per_device(): high = lax.ppermute(total[:13], 'space', fall)  16.5 us
    pallas_call x1, Pallas kernels, gather(): pl.pallas_call(functools.partial(gather_kernel, sizes), in_specs=[pl.Bloc...  8.05 us
    ppermute x1, starting transfers between devices, per_device(): got_up.append(lax.ppermute(ups[1], 'space', rise))  5.66 us
    ppermute x3, starting transfers between devices, over_vel(): lax.ppermute(values, 'vel', [(i, i ^ reach) for i in range(count)])  5.52 us
    ppermute x1, starting transfers between devices, per_device(): got_up = [lax.ppermute(ups[0], 'space', rise)]  4.53 us
    ppermute x3, waiting for transfers between devices, over_vel(): lax.ppermute(values, 'vel', [(i, i ^ reach) for i in range(count)])  3.75 us
    unnamed x13, local copies, waits for them, and re-layouts  3.59 us
  transfers between devices with their start and end apart: 9, of which 3 were waited for; matrix products, arithmetic and copies ran while one was open for 4% of the time, Pallas kernels for 30%

profile of v1, /device:TPU:1, one launch (start us, length us, event | category | flops | bytes accessed | tf_op | source)
XLA Modules:
  0.0 94.1 jit_solution(332685250107385081)
XLA Ops:
  0.6 8.1 %gather.1 = (f32[14,8,128]{2,1,0:T(8,128)}, f32[512,8,128]{2,1,0:T(8,128)}, f32[256,8,128]{2,1,0:T(8,128)}, f32[256,8,128]{2,1,0:T(8,128)}, f32[512,8,128]{2,1,0...) custom-call(s32[16]{0:T(128)} %bm_ref.5, f32[2048,8,128]{2,1,0:T(8,128)} %bitcast.24), custom_call_target="tpu_custom_call" | custom-call | tf_op jit(solution)/shard_map/gather/pallas_call | solution.py:170
  8.7 4.5 %collective-permute-start.9 = (f32[512,8,128]{2,1,0:T(8,128)}, f32[512,8,128]{2,1,0:T(8,128)S(1)}, u32[]{:S(2)}, u32[]{:S(2)}) collective-permute-start(f32[512,8,128]{2,1,0:T(8,128)} %get-tuple-element.31), channel_id=1, source_target_pairs={{0,1},{1,2},{2,3},{4,5},{5,6},{6,7},{8,9},{9,10},{10,11},{12,13},{... | collective-permute-start | bytes 6291464 | tf_op jit(solution)/shard_map/ppermute | solution.py:536
  13.2 1.9 %collective-permute-start.10 = (f32[512,8,128]{2,1,0:T(8,128)}, f32[512,8,128]{2,1,0:T(8,128)}, u32[]{:S(2)}, u32[]{:S(2)}) collective-permute-start(f32[512,8,128]{2,1,0:T(8,128)} %get-tuple-element.32), channel_id=1, source_target_pairs={{1,0},{2,1},{3,2},{5,4},{6,5},{7,6},{9,8},{10,9},{11,10},{13,12},{... | collective-permute-start | bytes 6291464 | tf_op jit(solution)/shard_map/ppermute | solution.py:537
  15.2 1.3 %collective-permute-start.2 = (f32[14,8,128]{2,1,0:T(8,128)}, f32[14,8,128]{2,1,0:T(8,128)S(1)}, u32[]{:S(2)}, u32[]{:S(2)}) collective-permute-start(f32[14,8,128]{2,1,0:T(8,128)} %get-tuple-element.23), channel_id=1, source_target_pairs={{0,4},{4,0},{8,12},{12,8},{16,20},{20,16},{24,28},{28,24},{1,5},{5... | collective-permute-start | bytes 172040 | tf_op jit(solution)/shard_map/ppermute | solution.py:511
  16.4 2.0 %collective-permute-done.2 = f32[14,8,128]{2,1,0:T(8,128)S(1)} collective-permute-done((f32[14,8,128]{2,1,0:T(8,128)}, f32[14,8,128]{2,1,0:T(8,128)S(1)}, u32[]{:S(2)}, u32[]{:S(2)}) %collective-permute-start.2) | collective-permute-done | bytes 57376 | tf_op jit(solution)/shard_map/ppermute | solution.py:511
  18.5 0.8 add.15
  19.3 1.3 %collective-permute-start.3 = (f32[14,8,128]{2,1,0:T(8,128)S(1)}, f32[14,8,128]{2,1,0:T(8,128)S(1)}, u32[]{:S(2)}, u32[]{:S(2)}) collective-permute-start(f32[14,8,128]{2,1,0:T(8,128)S(1)} %add.15), channel_id=1, source_target_pairs={{0,8},{4,12},{8,0},{12,4},{16,24},{20,28},{24,16},{28,20},{1,9},{5... | collective-permute-start | bytes 172040 | tf_op jit(solution)/shard_map/ppermute | solution.py:511
  20.6 1.7 %collective-permute-done.3 = f32[14,8,128]{2,1,0:T(8,128)S(1)} collective-permute-done((f32[14,8,128]{2,1,0:T(8,128)S(1)}, f32[14,8,128]{2,1,0:T(8,128)S(1)}, u32[]{:S(2)}, u32[]{:S(2)}) %collective-permute-start.3) | collective-permute-done | bytes 57376 | tf_op jit(solution)/shard_map/ppermute | solution.py:511
  22.3 2.9 %collective-permute-start.4 = (f32[14,8,128]{2,1,0:T(8,128)S(1)}, f32[14,8,128]{2,1,0:T(8,128)S(1)}, u32[]{:S(2)}, u32[]{:S(2)}) collective-permute-start(f32[14,8,128]{2,1,0:T(8,128)S(1)} %add.16), channel_id=1, source_target_pairs={{0,16},{4,20},{8,24},{12,28},{16,0},{20,4},{24,8},{28,12},{1,17},{... | collective-permute-start | bytes 172040 | tf_op jit(solution)/shard_map/ppermute | solution.py:511
  25.3 5.7 %collective-permute-start.7 = (f32[256,8,128]{2,1,0:T(8,128)}, f32[256,8,128]{2,1,0:T(8,128)S(1)}, u32[]{:S(2)}, u32[]{:S(2)}) collective-permute-start(f32[256,8,128]{2,1,0:T(8,128)} %get-tuple-element.25), channel_id=1, source_target_pairs={{0,1},{1,2},{2,3},{4,5},{5,6},{6,7},{8,9},{9,10},{10,11},{12,13},{... | collective-permute-start | bytes 3145736 | tf_op jit(solution)/shard_map/ppermute | solution.py:539
  31.0 0.5 slice.10
  32.2 1.9 %collective-permute-start.8 = (f32[256,8,128]{2,1,0:T(8,128)}, f32[256,8,128]{2,1,0:T(8,128)}, u32[]{:S(2)}, u32[]{:S(2)}) collective-permute-start(f32[256,8,128]{2,1,0:T(8,128)} %get-tuple-element.29), channel_id=1, source_target_pairs={{1,0},{2,1},{3,2},{5,4},{6,5},{7,6},{9,8},{10,9},{11,10},{13,12},{... | collective-permute-start | bytes 3145736 | tf_op jit(solution)/shard_map/ppermute | solution.py:540
  34.1 1.9 %collective-permute-start.6 = (f32[13,8,128]{2,1,0:T(8,128)S(1)}, f32[13,8,128]{2,1,0:T(8,128)S(1)}, u32[]{:S(2)}, u32[]{:S(2)}) collective-permute-start(f32[13,8,128]{2,1,0:T(8,128)S(1)} %slice.9), channel_id=1, source_target_pairs={{1,0},{2,1},{3,2},{5,4},{6,5},{7,6},{9,8},{10,9},{11,10},{13,12},{... | collective-permute-start | bytes 159752 | tf_op jit(solution)/shard_map/ppermute | solution.py:543
  36.0 16.5 %collective-permute-done.6.high_ref = f32[13,8,128]{2,1,0:T(8,128)S(1)} collective-permute-done((f32[13,8,128]{2,1,0:T(8,128)S(1)}, f32[13,8,128]{2,1,0:T(8,128)S(1)}, u32[]{:S(2)}, u32[]{:S(2)}) %collective-permute-start.6) | collective-permute-done | bytes 53280 | tf_op jit(solution)/shard_map/ppermute | solution.py:543
  52.6 1.9 %collective-permute-start.5 = (f32[13,8,128]{2,1,0:T(8,128)S(1)}, f32[13,8,128]{2,1,0:T(8,128)S(1)}, u32[]{:S(2)}, u32[]{:S(2)}) collective-permute-start(f32[13,8,128]{2,1,0:T(8,128)S(1)} %slice.9), channel_id=1, source_target_pairs={{0,1},{1,2},{2,3},{4,5},{5,6},{6,7},{8,9},{9,10},{10,11},{12,13},{... | collective-permute-start | bytes 159752 | tf_op jit(solution)/shard_map/ppermute | solution.py:542
  54.5 0.6 dynamic_slice.6
  57.1 0.6 copy-done.4
  57.7 2.1 %macro.1 = (f32[5,8,128]{2,1,0:T(8,128)}, f32[9,8,128]{2,1,0:T(8,128)}) custom-call(f32[13,8,128]{2,1,0:T(8,128)} %copy-done.4, f32[14,8,128]{2,1,0:T(8,128)} %copy-done.2, f32[13,8,128]{2,1,0:T(8,128)} %copy-done.3), custom_call_target="tpu_custom_call" | custom-call | tf_op jit(solution)/shard_map/macro/pallas_call | solution.py:303
  59.8 0.7 copy.15
  60.6 0.6 copy.18
  61.2 1.3 %copy-done = f32[512,8,128]{2,1,0:T(8,128)} copy-done((f32[512,8,128]{2,1,0:T(8,128)}, f32[512,8,128]{2,1,0:T(8,128)S(1)}, u32[]{:S(2)}) %copy-start) | copy-done | bytes 2097176
  62.5 25.7 %kinetic.2.refs_4_ = f32[2048,8,128]{2,1,0:T(8,128)} custom-call(s32[16]{0:T(128)} %bm_ref.5, f32[2]{0:T(128)} %scal_ref.3, f32[3]{0:T(128)} %drift_ref.3, s32[8,128]{1,0:T(8,128)} %bitcast.30, f32[9,8,128]{2,1,0:T(8,128)} %get-tuple-element.24.cell_ref, f32[2048,8,128]{2,1,0:T(8,128)} %bitcast.25, f32[512,8,128]{2,1,0:T(8,128)} %copy-done, ...), custom_call_target="tpu_custom_call" | custom-call | tf_op jit(solution)/shard_map/kinetic/pallas_call | solution.py:491
  88.3 1.0 %copy-done.1 = f32[256,8,128]{2,1,0:T(8,128)} copy-done((f32[256,8,128]{2,1,0:T(8,128)}, f32[256,8,128]{2,1,0:T(8,128)S(1)}, u32[]{:S(2)}) %copy-start.1) | copy-done | bytes 1048600
  89.3 4.8 %kinetic.3 = f32[2048,8,128]{2,1,0:T(8,128)} custom-call(s32[16]{0:T(128)} %bm_ref.5, f32[2]{0:T(128)} %scal_ref.3, f32[3]{0:T(128)} %drift_ref.3, s32[8,128]{1,0:T(8,128)} %bitcast.31, f32[9,8,128]{2,1,0:T(8,128)} %get-tuple-element.24.cell_ref, f32[2048,8,128]{2,1,0:T(8,128)} %bitcast.26, ...), custom_call_target="tpu_custom_call", output_to_operand_aliasing={{}: (10, {})} | custom-call | tf_op jit(solution)/shard_map/kinetic/pallas_call | solution.py:491
  (20 shorter events, 0.1 us)
Async XLA Ops:
  8.7 52.5 %collective-permute-start.9 = (f32[512,8,128]{2,1,0:T(8,128)}, f32[512,8,128]{2,1,0:T(8,128)S(1)}, u32[]{:S(2)}, u32[]{:S(2)}) collective-permute-start(f32[512,8,128]{2,1,0:T(8,128)} %get-tuple-element.31), channel_id=1, source_target_pairs={{0,1},{1,2},{2,3},{4,5},{5,6},{6,7},{8,9},{9,10},{10,11},{12,13},{... | collective-permute-start | bytes 6291464 | tf_op jit(solution)/shard_map/ppermute | solution.py:536
  13.2 47.9 %collective-permute-start.10 = (f32[512,8,128]{2,1,0:T(8,128)}, f32[512,8,128]{2,1,0:T(8,128)}, u32[]{:S(2)}, u32[]{:S(2)}) collective-permute-start(f32[512,8,128]{2,1,0:T(8,128)} %get-tuple-element.32), channel_id=1, source_target_pairs={{1,0},{2,1},{3,2},{5,4},{6,5},{7,6},{9,8},{10,9},{11,10},{13,12},{... | collective-permute-start | bytes 6291464 | tf_op jit(solution)/shard_map/ppermute | solution.py:537
  15.2 3.3 %collective-permute-start.2 = (f32[14,8,128]{2,1,0:T(8,128)}, f32[14,8,128]{2,1,0:T(8,128)S(1)}, u32[]{:S(2)}, u32[]{:S(2)}) collective-permute-start(f32[14,8,128]{2,1,0:T(8,128)} %get-tuple-element.23), channel_id=1, source_target_pairs={{0,4},{4,0},{8,12},{12,8},{16,20},{20,16},{24,28},{28,24},{1,5},{5... | collective-permute-start | bytes 172040 | tf_op jit(solution)/shard_map/ppermute | solution.py:511
  19.3 3.0 %collective-permute-start.3 = (f32[14,8,128]{2,1,0:T(8,128)S(1)}, f32[14,8,128]{2,1,0:T(8,128)S(1)}, u32[]{:S(2)}, u32[]{:S(2)}) collective-permute-start(f32[14,8,128]{2,1,0:T(8,128)S(1)} %add.15), channel_id=1, source_target_pairs={{0,8},{4,12},{8,0},{12,4},{16,24},{20,28},{24,16},{28,20},{1,9},{5... | collective-permute-start | bytes 172040 | tf_op jit(solution)/shard_map/ppermute | solution.py:511
  22.3 8.6 %collective-permute-start.4 = (f32[14,8,128]{2,1,0:T(8,128)S(1)}, f32[14,8,128]{2,1,0:T(8,128)S(1)}, u32[]{:S(2)}, u32[]{:S(2)}) collective-permute-start(f32[14,8,128]{2,1,0:T(8,128)S(1)} %add.16), channel_id=1, source_target_pairs={{0,16},{4,20},{8,24},{12,28},{16,0},{20,4},{24,8},{28,12},{1,17},{... | collective-permute-start | bytes 172040 | tf_op jit(solution)/shard_map/ppermute | solution.py:511
  25.3 63.0 %collective-permute-start.7 = (f32[256,8,128]{2,1,0:T(8,128)}, f32[256,8,128]{2,1,0:T(8,128)S(1)}, u32[]{:S(2)}, u32[]{:S(2)}) collective-permute-start(f32[256,8,128]{2,1,0:T(8,128)} %get-tuple-element.25), channel_id=1, source_target_pairs={{0,1},{1,2},{2,3},{4,5},{5,6},{6,7},{8,9},{9,10},{10,11},{12,13},{... | collective-permute-start | bytes 3145736 | tf_op jit(solution)/shard_map/ppermute | solution.py:539
  31.0 3.1 %copy-start.2 = (f32[14,8,128]{2,1,0:T(8,128)}, f32[14,8,128]{2,1,0:T(8,128)S(1)}, u32[]{:S(2)}) copy-start(f32[14,8,128]{2,1,0:T(8,128)S(1)} %add.17.own_ref) | copy-start | bytes 172036
  32.1 22.4 %copy-start.5 = (s32[8]{0:T(128)S(1)}, s32[8]{0:T(128)}, u32[]{:S(2)}) copy-start(s32[8]{0:T(128)} %param.11) | copy-start | bytes 100
  32.2 56.1 %collective-permute-start.8 = (f32[256,8,128]{2,1,0:T(8,128)}, f32[256,8,128]{2,1,0:T(8,128)}, u32[]{:S(2)}, u32[]{:S(2)}) collective-permute-start(f32[256,8,128]{2,1,0:T(8,128)} %get-tuple-element.29), channel_id=1, source_target_pairs={{1,0},{2,1},{3,2},{5,4},{6,5},{7,6},{9,8},{10,9},{11,10},{13,12},{... | collective-permute-start | bytes 3145736 | tf_op jit(solution)/shard_map/ppermute | solution.py:540
  34.1 18.5 %collective-permute-start.6 = (f32[13,8,128]{2,1,0:T(8,128)S(1)}, f32[13,8,128]{2,1,0:T(8,128)S(1)}, u32[]{:S(2)}, u32[]{:S(2)}) collective-permute-start(f32[13,8,128]{2,1,0:T(8,128)S(1)} %slice.9), channel_id=1, source_target_pairs={{1,0},{2,1},{3,2},{5,4},{6,5},{7,6},{9,8},{10,9},{11,10},{13,12},{... | collective-permute-start | bytes 159752 | tf_op jit(solution)/shard_map/ppermute | solution.py:543
  52.6 4.5 %copy-start.3 = (f32[13,8,128]{2,1,0:T(8,128)}, f32[13,8,128]{2,1,0:T(8,128)S(1)}, u32[]{:S(2)}) copy-start(f32[13,8,128]{2,1,0:T(8,128)S(1)} %collective-permute-done.6.high_ref) | copy-start | bytes 159748
  52.6 4.5 %collective-permute-start.5 = (f32[13,8,128]{2,1,0:T(8,128)S(1)}, f32[13,8,128]{2,1,0:T(8,128)S(1)}, u32[]{:S(2)}, u32[]{:S(2)}) collective-permute-start(f32[13,8,128]{2,1,0:T(8,128)S(1)} %slice.9), channel_id=1, source_target_pairs={{0,1},{1,2},{2,3},{4,5},{5,6},{6,7},{8,9},{9,10},{10,11},{12,13},{... | collective-permute-start | bytes 159752 | tf_op jit(solution)/shard_map/ppermute | solution.py:542
  57.1 0.6 copy-start.4
  61.2 1.4 %copy-start = (f32[512,8,128]{2,1,0:T(8,128)}, f32[512,8,128]{2,1,0:T(8,128)S(1)}, u32[]{:S(2)}) copy-start(f32[512,8,128]{2,1,0:T(8,128)S(1)} %collective-permute-done.9.refs_0_) | copy-start | bytes 6291460
  88.3 1.0 %copy-start.1 = (f32[256,8,128]{2,1,0:T(8,128)}, f32[256,8,128]{2,1,0:T(8,128)S(1)}, u32[]{:S(2)}) copy-start(f32[256,8,128]{2,1,0:T(8,128)S(1)} %collective-permute-done.7.refs_0_) | copy-start | bytes 3145732

commit v2 on v1

--- a/solution.py
+++ b/solution.py
@@ -30,8 +30,9 @@
 PARTS = NVY // ROWS
 SUB = 8
 LANES = 128
-VMEM_LIMIT = 60 << 20
-AHEAD = 4
+VMEM_LIMIT = 67_000_000
+SMALL_LIMIT = 16 << 20
+AHEAD = 16
 
 
 def speed(index, spacing):
@@ -169,8 +170,8 @@
     bufs = [jax.ShapeDtypeStruct((s * half, SUB, LANES), jnp.float32) for s in sizes if s]
     outs = pl.pallas_call(
         functools.partial(gather_kernel, sizes),
-        in_specs=[pl.BlockSpec(memory_space=pltpu.SMEM), pl.BlockSpec(memory_space=pl.ANY)],
-        out_specs=[pl.BlockSpec(memory_space=pltpu.VMEM)] + [pl.BlockSpec(memory_space=pl.ANY)] * (2 * len(bufs)),
+        in_specs=[pl.BlockSpec(memory_space=pltpu.SMEM), pl.BlockSpec(memory_space=pltpu.HBM)],
+        out_specs=[pl.BlockSpec(memory_space=pltpu.VMEM)] + [pl.BlockSpec(memory_space=pltpu.HBM)] * (2 * len(bufs)),
         out_shape=[jax.ShapeDtypeStruct((14, SUB, LANES), jnp.float32)] + bufs + bufs,
         scratch_shapes=[pltpu.VMEM((blocks * VB, SUB, LANES), jnp.float32),
                         pltpu.VMEM((blocks * half, SUB, LANES), jnp.float32),
@@ -225,16 +226,22 @@
     return fx, fy, fz
 
 
-def macro_kernel(low_ref, own_ref, high_ref, macro_ref, cell_ref):
+def macro_kernel(own_ref, other_ref, cross_ref, macro_ref, cell_ref):
     plane, spot, along_z = places()
     index = lax.axis_index("space")
+    even = (plane * 0 + index % 2) == 0
     count = lax.axis_size("space")
     first = (plane + index) == 0
     last = (plane + (count - 1 - index)) == 3
     last = jnp.logical_and(last, plane == 3)
     states, extras = [], []
-    for ref in (low_ref, own_ref, high_ref):
-        state, extra = convert([ref[r] for r in range(13)])
+    own = [own_ref[r] for r in range(13)]
+    other = [other_ref[r] for r in range(13)]
+    cross = [cross_ref[r] for r in range(13)]
+    low = [jnp.where(even, c, o) for c, o in zip(cross, other)]
+    high = [jnp.where(even, o, c) for c, o in zip(cross, other)]
+    for slab in (low, own, high):
+        state, extra = convert(slab)
         states.append(state)
         extras.append(extra)
 
@@ -299,13 +306,16 @@
     cell_ref[8] = 1.0 - rate
 
 
-def macro_solve(low, own, high):
+def macro_solve(own, other, cross):
+    vmem = pl.BlockSpec(memory_space=pltpu.VMEM)
     return pl.pallas_call(
         macro_kernel,
+        in_specs=[vmem] * 3,
+        out_specs=[vmem] * 2,
         out_shape=[jax.ShapeDtypeStruct((5, SUB, LANES), jnp.float32), jax.ShapeDtypeStruct((9, SUB, LANES), jnp.float32)],
-        compiler_params=pltpu.CompilerParams(vmem_limit_bytes=VMEM_LIMIT),
+        compiler_params=pltpu.CompilerParams(vmem_limit_bytes=SMALL_LIMIT),
         name="macro",
-    )(low, own, high)
+    )(own, other, cross)
 
 
 def kinetic_kernel(spans, aliased, bm_ref, scal_ref, drift_ref, mask_ref, cell_ref, f_hbm, *refs):
@@ -313,7 +323,7 @@
     up = refs[:kinds]
     down = refs[kinds:2 * kinds]
     refs = refs[2 * kinds + (1 if aliased else 0):]
-    out_hbm, fbuf, hbuf, gz_ref, az_ref, sz_ref, iz_ref, pick, in_sem, halo_sem, out_sem = refs
+    out_hbm, fbuf, hbuf, gz_ref, az_ref, sz_ref, iz_ref, turn_ref, yside_ref, zside_ref, pick, in_sem, halo_sem, out_sem = refs
     blocks = bm_ref.shape[0]
     low_slot = spans[0][0]
     high_slot = spans[-1][1]
@@ -362,6 +372,15 @@
 
     plane, spot, along_z = places()
     fixed = mask_ref[...] == 1
+    source = lax.broadcasted_iota(jnp.int32, (2 * LANES, LANES), 0) % LANES
+    target = lax.broadcasted_iota(jnp.int32, (2 * LANES, LANES), 1)
+    for step in (1, 2):
+        for sign in (0, 1):
+            away = step if sign else -step
+            wanted_y = (target + (away * NZ + LANES)) % LANES
+            wanted_z = target - target % NZ + (target % NZ + (away + NZ)) % NZ
+            for which, wanted in ((sign, wanted_y), (2 + sign, wanted_z)):
+                turn_ref[which, :, pl.ds((step - 1) * LANES, LANES)] = jnp.where(source == wanted, 1.0, 0.0).astype(jnp.bfloat16)
     ux, uy, uz, inv2t = cell_ref[0], cell_ref[1], cell_ref[2], cell_ref[3]
     hot = jnp.full((SUB, LANES), scal_ref[1], jnp.float32)
     hot_inv = 0.5 / hot
@@ -393,8 +412,21 @@
         ax = relx * cell_ref[5]
         offx = cx - drift_ref[0]
 
-        def rows(x_up, edge, y_up):
-            def body(y, carry):
+        x = fbuf[pl.ds(i * VB, VB)].reshape(VB * SUB, LANES)
+        hi = x.astype(jnp.bfloat16)
+        lo = (x - hi.astype(jnp.float32)).astype(jnp.bfloat16)
+        both = jnp.concatenate([hi, lo], axis=1)
+        yside_ref[...] = jnp.dot(both, turn_ref[jnp.where(y_positive, 0, 1)], preferred_element_type=jnp.float32)
+        both = both.reshape(ROWS, 2, NVZ * SUB // 2, 2 * LANES)
+        for side in (0, 1):
+            part = both[:, side].reshape(VB * SUB // 2, 2 * LANES)
+            zside_ref[side] = jnp.dot(part, turn_ref[3 - side], preferred_element_type=jnp.float32)
+
+        cross1 = jnp.where(y_positive, spot, LANES - 1 - spot) < NZ
+        cross2 = jnp.where(y_positive, spot, LANES - 1 - spot) < 2 * NZ
+
+        def rows(x_up, edge):
+            def one(y, carry):
                 cy = cy0 + y.astype(jnp.float32) * DY
                 k0y, k1y, k2y = upwind(KINETIC_STEP * jnp.abs(cy))
                 rely = cy - uy
@@ -426,41 +458,32 @@
                         x1 = sublane(-1)(jnp.where(plane == 0, halo, f))
                         x2 = sublane(-2)(jnp.where(plane < 2, halo, f))
                     total = total - k1x * x1 - k2x * x2
-                    across = sublane(4)(f)
-                    if y_up:
-                        y1 = lane(NZ)(jnp.where(spot >= LANES - NZ, across, f))
-                        y2 = lane(2 * NZ)(jnp.where(spot >= LANES - 2 * NZ, across, f))
-                    else:
-                        y1 = lane(-NZ)(jnp.where(spot < NZ, across, f))
-                        y2 = lane(-2 * NZ)(jnp.where(spot < 2 * NZ, across, f))
+                    lines = pl.ds((y * NVZ + e) * SUB, SUB)
+                    y1 = yside_ref[lines, :LANES]
+                    y2 = yside_ref[lines, LANES:]
+                    lines = pl.ds((y * (NVZ // 2) + e % (NVZ // 2)) * SUB, SUB)
+                    z1 = zside_ref[e // (NVZ // 2), lines, :LANES]
+                    z2 = zside_ref[e // (NVZ // 2), lines, LANES:]
+                    y1 = jnp.where(cross1, sublane(4)(y1), y1)
+                    y2 = jnp.where(cross2, sublane(4)(y2), y2)
                     total = total - k1y * y1 - k2y * y2
-                    if e >= NVZ // 2:
-                        wrap = lane(-NZ)(f)
-                        z1 = lane(1)(jnp.where(along_z == NZ - 1, wrap, f))
-                        z2 = lane(2)(jnp.where(along_z >= NZ - 2, wrap, f))
-                    else:
-                        wrap = lane(NZ)(f)
-                        z1 = lane(-1)(jnp.where(along_z == 0, wrap, f))
-                        z2 = lane(-2)(jnp.where(along_z < 2, wrap, f))
                     total = total - k1z * z1 - k2z * z2
                     shape = 1.0 + (axy + az_ref[e]) * (sxy + sz_ref[e])
                     total = total + (gxy * gz_ref[e]) * shape
                     fbuf[spot_v] = jnp.where(fixed, inflow, total)
                 return carry
 
-            lax.fori_loop(0, ROWS, body, 0)
+            lax.fori_loop(0, ROWS, one, 0)
 
         for x_up in (True, False):
             outer = (index == 0) if x_up else (index == count - 1)
             for edge in (True, False):
-                for y_up in (True, False):
-                    flag = jnp.logical_and(positive if x_up else jnp.logical_not(positive),
-                                           outer if edge else jnp.logical_not(outer))
-                    flag = jnp.logical_and(flag, y_positive if y_up else jnp.logical_not(y_positive))
-
-                    @pl.when(flag)
-                    def _(x_up=x_up, edge=edge, y_up=y_up):
-                        rows(x_up, edge, y_up)
+                flag = jnp.logical_and(positive if x_up else jnp.logical_not(positive),
+                                       outer if edge else jnp.logical_not(outer))
+
+                @pl.when(flag)
+                def _(x_up=x_up, edge=edge):
+                    rows(x_up, edge)
         pltpu.make_async_copy(fbuf.at[pl.ds(i * VB, VB)], out_hbm.at[pl.ds(i * VB, VB)], out_sem.at[i]).start()
         return carry
 
@@ -479,7 +502,7 @@
     half = VB // 2
     smem = pl.BlockSpec(memory_space=pltpu.SMEM)
     vmem = pl.BlockSpec(memory_space=pltpu.VMEM)
-    hbm = pl.BlockSpec(memory_space=pl.ANY)
+    hbm = pl.BlockSpec(memory_space=pltpu.HBM)
     operands = [block_map, scalars, drift, mask, cells, f, *up, *down]
     specs = [smem, smem, smem, vmem, vmem, hbm] + [hbm] * (len(up) + len(down))
     aliases = {}
@@ -494,7 +517,9 @@
         out_specs=hbm,
         out_shape=jax.ShapeDtypeStruct(f.shape, jnp.float32),
         scratch_shapes=[pltpu.VMEM((blocks * VB, SUB, LANES), jnp.float32), pltpu.VMEM((blocks * half, SUB, LANES), jnp.float32),
-                        table, table, table, table, pltpu.SMEM((2, blocks), jnp.int32),
+                        table, table, table, table, pltpu.VMEM((4, 2 * LANES, 2 * LANES), jnp.bfloat16),
+                        pltpu.VMEM((VB * SUB, 2 * LANES), jnp.float32), pltpu.VMEM((2, VB * SUB // 2, 2 * LANES), jnp.float32),
+                        pltpu.SMEM((2, blocks), jnp.int32),
                         pltpu.SemaphoreType.DMA((blocks,)), pltpu.SemaphoreType.DMA((blocks,)), pltpu.SemaphoreType.DMA((blocks,))],
         input_output_aliases=aliases,
         compiler_params=pltpu.CompilerParams(vmem_limit_bytes=VMEM_LIMIT),
@@ -535,13 +560,15 @@
     partial, ups, downs = gather(f, block_map, sizes)
     got_up = [lax.ppermute(ups[0], "space", rise)]
     got_down = [lax.ppermute(downs[0], "space", fall)]
+    total = over_vel(partial)
+    other = lax.ppermute(total, "space", [(i, i ^ 1) for i in range(space_count)])
+    cross = lax.ppermute(other, "space", [(i, i + 2) for i in range(0, space_count - 2, 2)]
+                         + [(i, i - 2) for i in range(3, space_count, 2)])
     if sizes[1]:
-        got_up.append(lax.ppermute(ups[1], "space", rise))
-        got_down.append(lax.ppermute(downs[1], "space", fall))
-    total = over_vel(partial)
-    low = lax.ppermute(total[:13], "space", rise)
-    high = lax.ppermute(total[:13], "space", fall)
-    macro, cells = macro_solve(low, total, high)
+        cross, up_next, down_next = lax.optimization_barrier((cross, ups[1], downs[1]))
+        got_up.append(lax.ppermute(up_next, "space", rise))
+        got_down.append(lax.ppermute(down_next, "space", fall))
+    macro, cells = macro_solve(total, other, cross)
     common = (f, block_map, inflow_scalars, inflow_drift, mask, cells)
     updated = kinetic(*common, ((0, sizes[0]),), got_up[:1], got_down[:1])
     if sizes[1]:

time: 95.4 us -> 72.3 us (0.76); the launches traced: 94.1 us -> 72 us
  waiting for transfers between devices: 20.3 us -> 9.89 us
  Pallas kernels: 40.7 us -> 32.9 us
  local copies, waits for them, and re-layouts: 5.45 us -> 2.33 us
    ppermute x4, waiting for transfers between devices: 16.6 us -> 4.17 us  [the longest x1 3.27 us: per_device(): lax.ppermute(other, 'space', [(i, i + 2) for i in range(0, space_count -...]
    pallas_call x2, Pallas kernels: 30.5 us -> 25.5 us  [kinetic(): pl.pallas_call(functools.partial(kinetic_kernel, spans, into is not None)...]
    unnamed x13 -> x5, local copies, waits for them, and re-layouts: 3.59 us -> 1.21 us
    ppermute x3, waiting for transfers between devices: 3.75 us -> 5.72 us  [over_vel(): lax.ppermute(values, 'vel', [(i, i ^ reach) for i in range(count)])]
    pallas_call x1, Pallas kernels: 2.11 us -> 0.64 us  [macro_solve(): pl.pallas_call(macro_kernel, in_specs=[vmem] * 3, out_specs=[vmem] * 2, o...]
    pallas_call x1, Pallas kernels: 8.05 us -> 6.84 us  [gather(): pl.pallas_call(functools.partial(gather_kernel, sizes), in_specs=[pl.Bloc...]
  transfers between devices with their start and end apart: 9 -> 9, of which waited for: 3 -> 5; matrix products, arithmetic and copies ran while one was open for 4% -> 4% of each run, Pallas kernels for 30% -> 30%
where the time goes in v2:
time: 72.3 us; the launch traced here: 72 us
  Pallas kernels  32.9 us (46%)
  starting transfers between devices  22.7 us (31%)
  waiting for transfers between devices  9.89 us (14%)
  between operations  3.36 us (5%)
  local copies, waits for them, and re-layouts  2.33 us (3%)
  other arithmetic  0.84 us (1%)
    pallas_call x2, Pallas kernels, kinetic(): pl.pallas_call(functools.partial(kinetic_kernel, spans, into is not None)...  25.5 us
    pallas_call x1, Pallas kernels, gather(): pl.pallas_call(functools.partial(gather_kernel, sizes), in_specs=[pl.Bloc...  6.84 us
    ppermute x3, waiting for transfers between devices, over_vel(): lax.ppermute(values, 'vel', [(i, i ^ reach) for i in range(count)])  5.72 us
    ppermute x3, starting transfers between devices, over_vel(): lax.ppermute(values, 'vel', [(i, i ^ reach) for i in range(count)])  5.43 us
    ppermute x1, starting transfers between devices, per_device(): got_up.append(lax.ppermute(up_next, 'space', rise))  5.36 us
    ppermute x1, starting transfers between devices, per_device(): got_up = [lax.ppermute(ups[0], 'space', rise)]  4.53 us
    ppermute x1, waiting for transfers between devices, per_device(): lax.ppermute(other, 'space', [(i, i + 2) for i in range(0, space_count -...  3.27 us
    ppermute x1, starting transfers between devices, per_device(): lax.ppermute(total, 'space', [(i, i ^ 1) for i in range(space_count)])  2.23 us
  transfers between devices with their start and end apart: 9, of which 5 were waited for; matrix products, arithmetic and copies ran while one was open for 4% of the time, Pallas kernels for 30%

profile of v2, /device:TPU:1, one launch (start us, length us, event | category | flops | bytes accessed | tf_op | source)
XLA Modules:
  0.0 72.0 jit_solution(14477352253430327557)
XLA Ops:
  0.6 6.8 %gather.1 = (f32[14,8,128]{2,1,0:T(8,128)}, f32[512,8,128]{2,1,0:T(8,128)}, f32[256,8,128]{2,1,0:T(8,128)}, f32[256,8,128]{2,1,0:T(8,128)}, f32[512,8,128]{2,1,0...) custom-call(s32[16]{0:T(128)} %bm_ref.5, f32[2048,8,128]{2,1,0:T(8,128)} %bitcast.25), custom_call_target="tpu_custom_call" | custom-call | tf_op jit(solution)/shard_map/gather/pallas_call | solution.py:171
  7.5 4.5 %collective-permute-start.9 = (f32[512,8,128]{2,1,0:T(8,128)}, f32[512,8,128]{2,1,0:T(8,128)}, u32[]{:S(2)}, u32[]{:S(2)}) collective-permute-start(f32[512,8,128]{2,1,0:T(8,128)} %get-tuple-element.37), channel_id=1, source_target_pairs={{0,1},{1,2},{2,3},{4,5},{5,6},{6,7},{8,9},{9,10},{10,11},{12,13},{... | collective-permute-start | bytes 6291464 | tf_op jit(solution)/shard_map/ppermute | solution.py:561
  12.0 1.9 %collective-permute-start.10 = (f32[512,8,128]{2,1,0:T(8,128)}, f32[512,8,128]{2,1,0:T(8,128)}, u32[]{:S(2)}, u32[]{:S(2)}) collective-permute-start(f32[512,8,128]{2,1,0:T(8,128)} %get-tuple-element.38), channel_id=1, source_target_pairs={{1,0},{2,1},{3,2},{5,4},{6,5},{7,6},{9,8},{10,9},{11,10},{13,12},{... | collective-permute-start | bytes 6291464 | tf_op jit(solution)/shard_map/ppermute | solution.py:562
  13.9 1.3 %collective-permute-start.2 = (f32[14,8,128]{2,1,0:T(8,128)}, f32[14,8,128]{2,1,0:T(8,128)S(1)}, u32[]{:S(2)}, u32[]{:S(2)}) collective-permute-start(f32[14,8,128]{2,1,0:T(8,128)} %get-tuple-element.26), channel_id=1, source_target_pairs={{0,4},{4,0},{8,12},{12,8},{16,20},{20,16},{24,28},{28,24},{1,5},{5... | collective-permute-start | bytes 172040 | tf_op jit(solution)/shard_map/ppermute | solution.py:536
  15.2 2.0 %collective-permute-done.2 = f32[14,8,128]{2,1,0:T(8,128)S(1)} collective-permute-done((f32[14,8,128]{2,1,0:T(8,128)}, f32[14,8,128]{2,1,0:T(8,128)S(1)}, u32[]{:S(2)}, u32[]{:S(2)}) %collective-permute-start.2) | collective-permute-done | bytes 57376 | tf_op jit(solution)/shard_map/ppermute | solution.py:536
  17.2 0.8 %add.15 = f32[14,8,128]{2,1,0:T(8,128)S(1)} add(f32[14,8,128]{2,1,0:T(8,128)} %get-tuple-element.26, f32[14,8,128]{2,1,0:T(8,128)S(1)} %collective-permute-done.2) | non-fusion elementwise | flops 14336 | bytes 172032 | tf_op jit(solution)/shard_map/add | solution.py:536
  18.1 2.0 %collective-permute-start.3 = (f32[14,8,128]{2,1,0:T(8,128)S(1)}, f32[14,8,128]{2,1,0:T(8,128)S(1)}, u32[]{:S(2)}, u32[]{:S(2)}) collective-permute-start(f32[14,8,128]{2,1,0:T(8,128)S(1)} %add.15), channel_id=1, source_target_pairs={{0,8},{4,12},{8,0},{12,4},{16,24},{20,28},{24,16},{28,20},{1,9},{5... | collective-permute-start | bytes 172040 | tf_op jit(solution)/shard_map/ppermute | solution.py:536
  20.0 1.9 %collective-permute-done.3 = f32[14,8,128]{2,1,0:T(8,128)S(1)} collective-permute-done((f32[14,8,128]{2,1,0:T(8,128)S(1)}, f32[14,8,128]{2,1,0:T(8,128)S(1)}, u32[]{:S(2)}, u32[]{:S(2)}) %collective-permute-start.3) | collective-permute-done | bytes 57376 | tf_op jit(solution)/shard_map/ppermute | solution.py:536
  21.9 2.2 %collective-permute-start.4 = (f32[14,8,128]{2,1,0:T(8,128)S(1)}, f32[14,8,128]{2,1,0:T(8,128)S(1)}, u32[]{:S(2)}, u32[]{:S(2)}) collective-permute-start(f32[14,8,128]{2,1,0:T(8,128)S(1)} %add.16), channel_id=1, source_target_pairs={{0,16},{4,20},{8,24},{12,28},{16,0},{20,4},{24,8},{28,12},{1,17},{... | collective-permute-start | bytes 172040 | tf_op jit(solution)/shard_map/ppermute | solution.py:536
  24.1 1.8 %collective-permute-done.4 = f32[14,8,128]{2,1,0:T(8,128)S(1)} collective-permute-done((f32[14,8,128]{2,1,0:T(8,128)S(1)}, f32[14,8,128]{2,1,0:T(8,128)S(1)}, u32[]{:S(2)}, u32[]{:S(2)}) %collective-permute-start.4) | collective-permute-done | bytes 57376 | tf_op jit(solution)/shard_map/ppermute | solution.py:536
  25.9 2.2 %collective-permute-start.5 = (f32[14,8,128]{2,1,0:T(8,128)S(1)}, f32[14,8,128]{2,1,0:T(8,128)S(1)}, u32[]{:S(2)}, u32[]{:S(2)}) collective-permute-start(f32[14,8,128]{2,1,0:T(8,128)S(1)} %add.17.own_ref), channel_id=1, source_target_pairs={{0,1},{1,0},{2,3},{3,2},{4,5},{5,4},{6,7},{7,6},{8,9},{9,8},{10,11... | collective-permute-start | bytes 172040 | tf_op jit(solution)/shard_map/ppermute | solution.py:564
  28.2 0.9 %collective-permute-done.5.other_ref = f32[14,8,128]{2,1,0:T(8,128)S(1)} collective-permute-done((f32[14,8,128]{2,1,0:T(8,128)S(1)}, f32[14,8,128]{2,1,0:T(8,128)S(1)}, u32[]{:S(2)}, u32[]{:S(2)}) %collective-permute-start.5) | collective-permute-done | bytes 57376 | tf_op jit(solution)/shard_map/ppermute | solution.py:564
  29.1 1.3 %collective-permute-start.6 = (f32[14,8,128]{2,1,0:T(8,128)S(1)}, f32[14,8,128]{2,1,0:T(8,128)S(1)}, u32[]{:S(2)}, u32[]{:S(2)}) collective-permute-start(f32[14,8,128]{2,1,0:T(8,128)S(1)} %collective-permute-done.5.other_ref), channel_id=1, source_target_pairs={{0,2},{3,1},{4,6},{7,5},{8,10},{11,9},{12,14},{15,13},{16,18},{19,... | collective-permute-start | bytes 172040 | tf_op jit(solution)/shard_map/ppermute | solution.py:565
  30.3 0.5 slice.4
  31.5 0.0 copy-start.1
  31.5 3.3 %collective-permute-done.6.cross_ref = f32[14,8,128]{2,1,0:T(8,128)S(1)} collective-permute-done((f32[14,8,128]{2,1,0:T(8,128)S(1)}, f32[14,8,128]{2,1,0:T(8,128)S(1)}, u32[]{:S(2)}, u32[]{:S(2)}) %collective-permute-start.6) | collective-permute-done | bytes 57376 | tf_op jit(solution)/shard_map/ppermute | solution.py:565
  34.8 5.4 %collective-permute-start.7 = (f32[256,8,128]{2,1,0:T(8,128)}, f32[256,8,128]{2,1,0:T(8,128)}, u32[]{:S(2)}, u32[]{:S(2)}) collective-permute-start(f32[256,8,128]{2,1,0:T(8,128)} %get-tuple-element.31), channel_id=1, source_target_pairs={{0,1},{1,2},{2,3},{4,5},{5,6},{6,7},{8,9},{9,10},{10,11},{12,13},{... | collective-permute-start | bytes 3145736 | tf_op jit(solution)/shard_map/ppermute | solution.py:569
  40.2 1.9 %collective-permute-start.8 = (f32[256,8,128]{2,1,0:T(8,128)}, f32[256,8,128]{2,1,0:T(8,128)}, u32[]{:S(2)}, u32[]{:S(2)}) collective-permute-start(f32[256,8,128]{2,1,0:T(8,128)} %get-tuple-element.35), channel_id=1, source_target_pairs={{1,0},{2,1},{3,2},{5,4},{6,5},{7,6},{9,8},{10,9},{11,10},{13,12},{... | collective-permute-start | bytes 3145736 | tf_op jit(solution)/shard_map/ppermute | solution.py:570
  42.1 0.6 dynamic_slice.6
  44.7 0.6 macro.1
  45.3 0.6 copy-done
  46.0 0.6 copy.18
  46.6 20.9 %kinetic.2.refs_4_ = f32[2048,8,128]{2,1,0:T(8,128)} custom-call(s32[16]{0:T(128)} %bm_ref.5, f32[2]{0:T(128)} %scal_ref.3, f32[3]{0:T(128)} %drift_ref.3, s32[8,128]{1,0:T(8,128)} %bitcast.30, f32[9,8,128]{2,1,0:T(8,128)} %copy-done, f32[2048,8,128]{2,1,0:T(8,128)} %bitcast.26, f32[512,8,128]{2,1,0:T(8,128)} %collective-permute-done.9.refs_0_, ...), custom_call_target="tpu_custom_call" | custom-call | tf_op jit(solution)/shard_map/kinetic/pallas_call | solution.py:514
  67.5 4.6 %kinetic.3 = f32[2048,8,128]{2,1,0:T(8,128)} custom-call(s32[16]{0:T(128)} %bm_ref.5, f32[2]{0:T(128)} %scal_ref.3, f32[3]{0:T(128)} %drift_ref.3, s32[8,128]{1,0:T(8,128)} %bitcast.31, f32[9,8,128]{2,1,0:T(8,128)} %copy-done, f32[2048,8,128]{2,1,0:T(8,128)} %bitcast.27, ...), custom_call_target="tpu_custom_call", output_to_operand_aliasing={{}: (10, {})} | custom-call | tf_op jit(solution)/shard_map/kinetic/pallas_call | solution.py:514
  (11 shorter events, 0.1 us)
Async XLA Ops:
  7.5 39.1 %collective-permute-start.9 = (f32[512,8,128]{2,1,0:T(8,128)}, f32[512,8,128]{2,1,0:T(8,128)}, u32[]{:S(2)}, u32[]{:S(2)}) collective-permute-start(f32[512,8,128]{2,1,0:T(8,128)} %get-tuple-element.37), channel_id=1, source_target_pairs={{0,1},{1,2},{2,3},{4,5},{5,6},{6,7},{8,9},{9,10},{10,11},{12,13},{... | collective-permute-start | bytes 6291464 | tf_op jit(solution)/shard_map/ppermute | solution.py:561
  12.0 34.5 %collective-permute-start.10 = (f32[512,8,128]{2,1,0:T(8,128)}, f32[512,8,128]{2,1,0:T(8,128)}, u32[]{:S(2)}, u32[]{:S(2)}) collective-permute-start(f32[512,8,128]{2,1,0:T(8,128)} %get-tuple-element.38), channel_id=1, source_target_pairs={{1,0},{2,1},{3,2},{5,4},{6,5},{7,6},{9,8},{10,9},{11,10},{13,12},{... | collective-permute-start | bytes 6291464 | tf_op jit(solution)/shard_map/ppermute | solution.py:562
  13.9 3.3 %collective-permute-start.2 = (f32[14,8,128]{2,1,0:T(8,128)}, f32[14,8,128]{2,1,0:T(8,128)S(1)}, u32[]{:S(2)}, u32[]{:S(2)}) collective-permute-start(f32[14,8,128]{2,1,0:T(8,128)} %get-tuple-element.26), channel_id=1, source_target_pairs={{0,4},{4,0},{8,12},{12,8},{16,20},{20,16},{24,28},{28,24},{1,5},{5... | collective-permute-start | bytes 172040 | tf_op jit(solution)/shard_map/ppermute | solution.py:536
  18.1 3.9 %collective-permute-start.3 = (f32[14,8,128]{2,1,0:T(8,128)S(1)}, f32[14,8,128]{2,1,0:T(8,128)S(1)}, u32[]{:S(2)}, u32[]{:S(2)}) collective-permute-start(f32[14,8,128]{2,1,0:T(8,128)S(1)} %add.15), channel_id=1, source_target_pairs={{0,8},{4,12},{8,0},{12,4},{16,24},{20,28},{24,16},{28,20},{1,9},{5... | collective-permute-start | bytes 172040 | tf_op jit(solution)/shard_map/ppermute | solution.py:536
  21.9 4.0 %collective-permute-start.4 = (f32[14,8,128]{2,1,0:T(8,128)S(1)}, f32[14,8,128]{2,1,0:T(8,128)S(1)}, u32[]{:S(2)}, u32[]{:S(2)}) collective-permute-start(f32[14,8,128]{2,1,0:T(8,128)S(1)} %add.16), channel_id=1, source_target_pairs={{0,16},{4,20},{8,24},{12,28},{16,0},{20,4},{24,8},{28,12},{1,17},{... | collective-permute-start | bytes 172040 | tf_op jit(solution)/shard_map/ppermute | solution.py:536
  25.9 3.1 %collective-permute-start.5 = (f32[14,8,128]{2,1,0:T(8,128)S(1)}, f32[14,8,128]{2,1,0:T(8,128)S(1)}, u32[]{:S(2)}, u32[]{:S(2)}) collective-permute-start(f32[14,8,128]{2,1,0:T(8,128)S(1)} %add.17.own_ref), channel_id=1, source_target_pairs={{0,1},{1,0},{2,3},{3,2},{4,5},{5,4},{6,7},{7,6},{8,9},{9,8},{10,11... | collective-permute-start | bytes 172040 | tf_op jit(solution)/shard_map/ppermute | solution.py:564
  29.1 5.8 %collective-permute-start.6 = (f32[14,8,128]{2,1,0:T(8,128)S(1)}, f32[14,8,128]{2,1,0:T(8,128)S(1)}, u32[]{:S(2)}, u32[]{:S(2)}) collective-permute-start(f32[14,8,128]{2,1,0:T(8,128)S(1)} %collective-permute-done.5.other_ref), channel_id=1, source_target_pairs={{0,2},{3,1},{4,6},{7,5},{8,10},{11,9},{12,14},{15,13},{16,18},{19,... | collective-permute-start | bytes 172040 | tf_op jit(solution)/shard_map/ppermute | solution.py:565
  31.5 10.6 %copy-start.1 = (s32[8]{0:T(128)S(1)}, s32[8]{0:T(128)}, u32[]{:S(2)}) copy-start(s32[8]{0:T(128)} %param.11) | copy-start | bytes 100
  34.8 32.6 %collective-permute-start.7 = (f32[256,8,128]{2,1,0:T(8,128)}, f32[256,8,128]{2,1,0:T(8,128)}, u32[]{:S(2)}, u32[]{:S(2)}) collective-permute-start(f32[256,8,128]{2,1,0:T(8,128)} %get-tuple-element.31), channel_id=1, source_target_pairs={{0,1},{1,2},{2,3},{4,5},{5,6},{6,7},{8,9},{9,10},{10,11},{12,13},{... | collective-permute-start | bytes 3145736 | tf_op jit(solution)/shard_map/ppermute | solution.py:569
  40.2 27.3 %collective-permute-start.8 = (f32[256,8,128]{2,1,0:T(8,128)}, f32[256,8,128]{2,1,0:T(8,128)}, u32[]{:S(2)}, u32[]{:S(2)}) collective-permute-start(f32[256,8,128]{2,1,0:T(8,128)} %get-tuple-element.35), channel_id=1, source_target_pairs={{1,0},{2,1},{3,2},{5,4},{6,5},{7,6},{9,8},{10,9},{11,10},{13,12},{... | collective-permute-start | bytes 3145736 | tf_op jit(solution)/shard_map/ppermute | solution.py:570
  45.3 0.6 copy-start
